TPU v7x, 32 devices: a whole 2x2x4 slice. The times are simulated.
32 devices in a mesh: ep: 8 (over z, y), dp: 4 (over x, core).
Axes of the slice: x: 2, y: 2, z: 4, core: 2. Of those that a mesh axis runs over, the one named last changes fastest.
Arguments:
- tokens: bfloat16 [6144, 2880], P(('ep', 'dp')), may hold values from -64 to 64
- out_grad: bfloat16 [6144, 2880], P(('ep', 'dp')), may hold values from -6 to 6
- indices: int32 [6144, 4], P(('ep', 'dp')), may hold values from 0 to 31, as said below
- expert_rows: bfloat16 [4, 32, 8, 36, 2880], P('dp', 'ep'), may hold values from -0.111328125 to 0.111328125
- router_weight: bfloat16 [2880, 32], replicated, may hold values from -1 to 1
- router_bias: float32 [32], replicated, may hold values from -3 to 3
- balance_scale: float32 [1], replicated, may hold values from 64 to 256
Outputs:
- token_grad: bfloat16 [6144, 2880], P(('ep', 'dp'))
- weight_grad: float32 [2880, 32], P('dp', 'ep')
- balance_loss: float32 [1], replicated
Inputs may be any that keep to these rules, and one draw needn't show every extreme that they name: `indices`: each row names 4 different experts. Within the 192 rows of one device no expert is named by more than 36 rows, and some expert is named by exactly 36 rows. Within the rows of one device the 4 experts of one ep index (experts j * 4 to j * 4 + 3) are named by at most 108 rows together, and those of some ep index by exactly 108. Every expert is named by some row of every device.
All inputs are finite; a program needn't handle non-finite values.
Results may differ from a plain program's by a relative error of at most 0.0014.
The roundings to bfloat16 on the way count: a program that leaves them out, or rounds other values in their place, can miss the bound.
Values may be sent and summed in bfloat16 or wider, within the bound.
A program may use at most 128 MiB of HBM per device.

v0:
```python
import functools
import math

import jax
import jax.numpy as jnp
from jax import lax
from jax.experimental import pallas as pl
from jax.experimental.pallas import tpu as pltpu
from jax.sharding import PartitionSpec as P

MESH = pl.DeviceIdType.MESH
F32 = jnp.float32
BF16 = jnp.bfloat16
CHUNK = 768


def dot_nt(x, y, precision=None):
    return lax.dot_general(
        x, y, (((1,), (1,)), ((), ())), preferred_element_type=F32, precision=precision
    )


def dot_nn(x, y, precision=None):
    return lax.dot_general(
        x, y, (((1,), (0,)), ((), ())), preferred_element_type=F32, precision=precision
    )


def kernel(cfg, *refs):
    ep, dp, tok_dev, chosen, experts, exp_dev, cap, packed, widths, token_total = cfg
    line = ep // 2
    chunks = len(widths)
    starts = [sum(widths[:c]) for c in range(chunks)]
    (idx_in, grad_in, rows_in, tok_in, wt_in, bias_in, scale_in, lg_out, wg_out, loss_out) = refs[:10]
    refs = refs[10:]
    xb = refs[:chunks]
    lsend = refs[chunks:2 * chunks]
    lrecv = refs[2 * chunks:3 * chunks]
    rows_v = refs[3 * chunks:4 * chunks]
    back = refs[4 * chunks:5 * chunks]
    (rows_raw, piled, tgt_r, acc_r, s_back, r_back, idx_all, pin, pout, tgt_x, tgt_p, acc_x, acc_p, rst, rbuf, tks, tkr, logit_v, prob_v,
     named_v, st_dp, st_ep, lgd, ws, wr,
     s_rows, s_own, s_idx, r_idx, s_right, s_left, r_x, s_leaf, r_leaf, s_rep, r_rep,
     s_tk, r_tk, s_sd, r_sd, s_se, r_se, s_lg, r_lg, s_w, r_w) = refs[5 * chunks:]
    me = lax.axis_index("ep")
    md = lax.axis_index("dp")
    pos = me // 2
    side = lax.rem(me, 2)
    mate = pos * 2 + 1 - side
    swapped = range(min(1, chunks - 1)) if line >= 4 else range(0)
    last = line - 1
    at_end = jnp.logical_or(pos == 0, pos == last)
    near_end = jnp.logical_or(pos == 1, pos == last - 1)
    end = jnp.where(pos * 2 < line, 0, last)
    near = jnp.where(pos * 2 < line, 1, last - 1)

    def ep_id(other):
        return (other, md)

    def remote(src, dst, s, r, dev):
        return pltpu.make_async_remote_copy(
            src_ref=src, dst_ref=dst, send_sem=s, recv_sem=r, device_id=dev, device_id_type=MESH
        )

    def ep_peer(s):
        return lax.rem(me + s, ep)

    def dp_peer(s):
        return lax.rem(md + s, dp)

    own = [
        pltpu.make_async_copy(grad_in.at[:, pl.ds(starts[c], widths[c])], xb[c].at[pos], s_own.at[c])
        for c in range(chunks)
    ]
    for copy in own:
        copy.start()
    rows_copy = pltpu.make_async_copy(rows_in, rows_raw, s_rows)
    rows_copy.start()

    barrier = pltpu.get_barrier_semaphore()

    def greet(s, carry):
        pl.semaphore_signal(barrier, inc=1, device_id=ep_id(ep_peer(s)), device_id_type=MESH)
        return carry

    lax.fori_loop(1, ep, greet, 0)
    for s in range(1, dp):
        pl.semaphore_signal(barrier, inc=1, device_id=(me, dp_peer(s)), device_id_type=MESH)
    pl.semaphore_wait(barrier, ep - 1 + dp - 1)

    def idx_copy(s):
        return remote(idx_in, idx_all.at[me], s_idx.at[s], r_idx.at[me], ep_id(ep_peer(s)))

    def idx_arrival(s):
        src = lax.rem(me + ep - s, ep)
        return remote(idx_in, idx_all.at[src], s_idx.at[s], r_idx.at[src], ep_id(src))

    def loop_ep(fn):
        def body(s, carry):
            fn(s)
            return carry
        lax.fori_loop(1, ep, body, 0)

    def to_right(q, c):
        return remote(xb[c].at[q], xb[c].at[q], s_right.at[q, c], r_x.at[q, c], ep_id(me + 2))

    def to_left(q, c):
        return remote(xb[c].at[q], xb[c].at[q], s_left.at[q, c], r_x.at[q, c], ep_id(me - 2))

    def leaf(q, c):
        return remote(lsend[c].at[q], lrecv[c].at[q], s_leaf.at[q, c], r_leaf.at[q, c], ep_id(mate))

    def send_back(b, c):
        return remote(rows_v[c].at[near * 2 + b], back[c].at[side], s_back.at[b, c], r_back.at[side, c], ep_id(near * 2 + b))

    def from_left(s, c):
        ok = pos - s >= 0
        return jnp.logical_and(ok, pos < last) if s == 1 and c in swapped else ok

    def from_right(s, c):
        ok = pos + s < line
        return jnp.logical_and(ok, pos > 0) if s == 1 and c in swapped else ok

    def reply(j):
        return remote(rst.at[j], rbuf.at[me], s_rep.at[j], r_rep.at[me], ep_id(j))

    loop_ep(lambda s: idx_copy(s).start())
    for c in range(chunks):
        own[c].wait()

        @pl.when(pos < last - (c in swapped))
        def _():
            to_right(pos, c).start()

        @pl.when(pos > 0 + (c in swapped))
        def _():
            to_left(pos, c).start()

    part = tok_in.shape[1] // dp
    for d in range(dp):
        tks[d] = tok_in[:, d * part:(d + 1) * part]

    idx = idx_in[...]
    expert_row = lax.broadcasted_iota(jnp.int32, (experts, tok_dev), 0)
    named = jnp.zeros((experts, tok_dev), F32)
    for k in range(chosen):
        named = named + jnp.where(idx[k:k + 1, :] == expert_row, 1.0, 0.0)
    eye_r = lax.broadcasted_iota(jnp.int32, (experts, experts), 0)
    eye_c = lax.broadcasted_iota(jnp.int32, (experts, experts), 1)

    def upright(line_of):
        return jnp.sum(jnp.where(eye_r == eye_c, line_of, 0.0), axis=1, keepdims=True)

    logits = dot_nt(wt_in[...], tok_in[...]) + upright(bias_in[...])
    top = jnp.max(logits, axis=0, keepdims=True)
    power = jnp.exp(logits - top)
    prob = power / jnp.sum(power, axis=0, keepdims=True)
    logit_v[...] = logits
    prob_v[...] = prob
    named_v[...] = named
    ones = jnp.ones((8, tok_dev), F32)
    count_row = dot_nt(ones, named, lax.Precision.HIGHEST)
    prob_row = dot_nt(ones, prob, lax.Precision.HIGHEST)
    stat_row = lax.broadcasted_iota(jnp.int32, (8, experts), 0)
    st_dp[md] = jnp.where(stat_row == 0, count_row, prob_row)

    def tk_copy(s):
        return remote(tks.at[dp_peer(s)], tkr.at[md], s_tk.at[s], r_tk.at[md], (me, dp_peer(s)))

    def tk_arrival(s):
        src = lax.rem(md + dp - s, dp)
        return remote(tks.at[src], tkr.at[src], s_tk.at[s], r_tk.at[src], (me, src))

    def sd_copy(s):
        return remote(st_dp.at[md], st_dp.at[md], s_sd.at[s], r_sd.at[md], (me, dp_peer(s)))

    def sd_arrival(s):
        src = lax.rem(md + dp - s, dp)
        return remote(st_dp.at[src], st_dp.at[src], s_sd.at[s], r_sd.at[src], (me, src))

    for s in range(1, dp):
        sd_copy(s).start()
    for s in range(1, dp):
        tk_copy(s).start()
    tkr[md] = tks[md]

    t_from = lax.broadcasted_iota(jnp.int32, (tok_dev, tok_dev), 0)
    t_to = lax.broadcasted_iota(jnp.int32, (tok_dev, tok_dev), 1)
    upper = jnp.where(t_from < t_to, 1.0, 0.0).astype(BF16)
    row8 = lax.broadcasted_iota(jnp.int32, (8, tok_dev), 0)
    slot_p = lax.broadcasted_iota(jnp.int32, (packed, tok_dev), 0).astype(F32)

    def plan(table, group):
        who = jnp.where(row8 < exp_dev, group * exp_dev + row8, -2)
        hit = jnp.zeros((8, tok_dev), F32)
        for k in range(chosen):
            hit = hit + jnp.where(table[k:k + 1, :] == who, 1.0, 0.0)
        need = jnp.max(hit, axis=0, keepdims=True)
        stack = jnp.where(row8 == exp_dev, need, hit)
        before = dot_nn(stack.astype(BF16), upper)
        place = jnp.where(need > 0.5, before[exp_dev:exp_dev + 1, :], -1.0)
        target = jnp.where(hit > 0.5, before, -1.0)
        pack = jnp.where(slot_p == place, 1.0, 0.0).astype(BF16)
        return target, pack

    idx_all[me] = idx
    loop_ep(lambda s: idx_arrival(s).wait_recv())

    def plans(q, carry):
        table = idx_all[q * 2 + side]
        target, _ = plan(table, me)
        tgt_x[q] = target
        _, pack = plan(table, mate)
        pout[q] = pack
        target, pack = plan(idx_all[q * 2 + 1 - side], me)
        pin[q] = pack
        tgt_p[q] = dot_nt((target + 1.0).astype(BF16), pack) - 1.0
        acc_x[q] = jnp.zeros((8, tok_dev), F32)
        acc_p[q] = jnp.zeros((8, packed), F32)
        return carry

    lax.fori_loop(0, line, plans, 0)
    for b in range(2):
        tgt_r[b], _ = plan(idx, end * 2 + b)
        acc_r[b] = jnp.zeros((8, tok_dev), F32)
    rows_copy.wait()

    deep = piled.shape[1] // ep
    slot_r = lax.broadcasted_iota(jnp.int32, (deep, cap * ep), 0)
    lies = lax.broadcasted_iota(jnp.int32, (deep, cap * ep), 1)
    order = jnp.concatenate(
        [jnp.where(jnp.logical_and(lies == slot_r * ep + j, slot_r < cap), 1.0, 0.0) for j in range(ep)], axis=0
    ).astype(BF16)
    spare = rows_v[0].shape[1] - exp_dev * cap

    def sort_rows(c):
        w = widths[c]
        for e in range(exp_dev):
            piled[e, :, 0:w] = dot_nn(order, rows_raw[e, :, starts[c]:starts[c] + w])

        def put(j, carry):
            at = pl.ds(pl.multiple_of(j * deep, 8), deep)
            pieces = [piled[e, at, 0:w][0:cap, :] for e in range(exp_dev)]
            if spare:
                pieces.append(jnp.zeros((spare, w), F32))
            rows_v[c][j] = jnp.concatenate(pieces, axis=0).astype(BF16)
            return carry

        lax.fori_loop(0, ep, put, 0)

    def gathered(table, block, target, count):
        height = table.shape[0]
        slot = lax.broadcasted_iota(jnp.int32, (height, count), 0).astype(F32)
        row = lax.broadcasted_iota(jnp.int32, (8, count), 0)
        dots = dot_nt(table, block)
        out = jnp.zeros((8, count), F32)
        for e in range(exp_dev):
            want = jnp.where(target[e:e + 1, :] >= 0.0, target[e:e + 1, :] + e * cap, -1.0)
            one = jnp.sum(jnp.where(slot == want, dots, 0.0), axis=0, keepdims=True)
            out = jnp.where(row == e, one, out)
        return out

    def give_leaf(q, c):
        lsend[c][q] = dot_nn(pout[q], xb[c][q]).astype(BF16)
        leaf(q, c).start()

    def use_block(q, c):
        acc_x[q] += gathered(rows_v[c][q * 2 + side], xb[c][q], tgt_x[q], tok_dev)

    def use_leaf(q, c):
        leaf(q, c).wait_recv()
        acc_p[q] += gathered(rows_v[c][q * 2 + 1 - side], lrecv[c][q], tgt_p[q], packed)

    def answer(j, value):
        rst[j] = value
        reply(j).start()

    def done_block(q):
        answer(q * 2 + side, acc_x[q])

    def done_leaf(q):
        answer(q * 2 + 1 - side, dot_nn(acc_p[q], pin[q].astype(F32), lax.Precision.HIGHEST))

    def leaf_step(s, c):
        def go(q):
            use_leaf(q, c)
            if c == chunks - 1:
                done_leaf(q)
        if s == 0:
            go(pos)
            return

        @pl.when(from_left(s, c))
        def _():
            go(pos - s)

        @pl.when(from_right(s, c))
        def _():
            go(pos + s)

    lag = 2
    steps = [(s, c) for s in range(line) for c in range(chunks)]
    for n, (s, c) in enumerate(steps):
        if s == 0:
            give_leaf(pos, c)
            sort_rows(c)
            if c in swapped:
                @pl.when(at_end)
                def _():
                    for b in range(2):
                        send_back(b, c).start()
            use_block(pos, c)
            if c == chunks - 1:
                rbuf[me] = acc_x[pos]
        else:
            @pl.when(from_left(s, c))
            def _():
                q = pos - s
                to_right(q, c).wait_recv()

                @pl.when(pos < line - 1)
                def _():
                    to_right(q, c).start()

            @pl.when(from_right(s, c))
            def _():
                q = pos + s
                to_left(q, c).wait_recv()

                @pl.when(pos > 0)
                def _():
                    to_left(q, c).start()

            for q, ok in ((pos - s, from_left(s, c)), (pos + s, from_right(s, c))):
                @pl.when(ok)
                def _(q=q):
                    give_leaf(q, c)

            for q, ok in ((pos - s, from_left(s, c)), (pos + s, from_right(s, c))):
                @pl.when(ok)
                def _(q=q):
                    use_block(q, c)
                    if c == chunks - 1:
                        done_block(q)
        if n >= lag:
            leaf_step(*steps[n - lag])
        if s == last and c in swapped:
            @pl.when(near_end)
            def _():
                for b in range(2):
                    remote(back[c].at[b], back[c].at[b], s_back.at[b, c], r_back.at[b, c], ep_id(end * 2 + b)).wait_recv()
                    acc_r[b] += gathered(back[c][b], xb[c][pos], tgt_r[b], tok_dev)
        if n == 1:
            for s_ in range(1, dp):
                sd_arrival(s_).wait_recv()
            total = st_dp[0]
            for d in range(1, dp):
                total = total + st_dp[d]
            st_ep[me] = total
            loop_ep(lambda s_: remote(st_ep.at[me], st_ep.at[me], s_se.at[s_], r_se.at[me], ep_id(ep_peer(s_))).start())
    for n in range(len(steps) - lag, len(steps)):
        leaf_step(*steps[n])

    def se_arrival(s_):
        src = lax.rem(me + ep - s_, ep)
        remote(st_ep.at[src], st_ep.at[src], s_se.at[s_], r_se.at[src], ep_id(src)).wait_recv()

    loop_ep(se_arrival)
    stats = lax.fori_loop(1, ep, lambda j, acc: acc + st_ep[j], st_ep[0])
    share = stats[0:1, :] / (token_total * chosen)
    mean = stats[1:2, :] / token_total
    loss_out[...] = experts * jnp.sum(share * mean, axis=1, keepdims=True)
    push_row = scale_in[0] * experts * share
    push = upright(push_row)
    prob = prob_v[...]
    spread = prob * (push - jnp.sum(prob * push, axis=0, keepdims=True))
    named = named_v[...]
    logits = logit_v[...]
    high = jnp.max(jnp.where(named > 0.5, logits, -jnp.inf), axis=0, keepdims=True)
    mix = jnp.where(named > 0.5, jnp.exp(jnp.minimum(logits - high, 0.0)), 0.0)
    mix = mix / jnp.sum(mix, axis=0, keepdims=True)

    def rep_arrival(s_):
        src = lax.rem(me + ep - s_, ep)
        remote(rst.at[src], rbuf.at[src], s_rep.at[src], r_rep.at[src], ep_id(src)).wait_recv()

    loop_ep(rep_arrival)
    if len(swapped):
        @pl.when(near_end)
        def _():
            for b in range(2):
                rbuf[end * 2 + b] += acc_r[b]
    dots = jnp.concatenate([rbuf[j, 0:exp_dev, :] for j in range(ep)], axis=0)
    sel = mix * (dots - jnp.sum(mix * dots, axis=0, keepdims=True))
    grad = (spread + sel).astype(BF16)
    lg_out[...] = grad
    lgd[md] = grad

    def lg_copy(s):
        return remote(lgd.at[md], lgd.at[md], s_lg.at[s], r_lg.at[md], (me, dp_peer(s)))

    def lg_arrival(s):
        src = lax.rem(md + dp - s, dp)
        return remote(lgd.at[src], lgd.at[src], s_lg.at[s], r_lg.at[src], (me, src))

    for s in range(1, dp):
        lg_copy(s).start()
    for s in range(1, dp):
        tk_arrival(s).wait_recv()
    for s in range(1, dp):
        lg_arrival(s).wait_recv()
    term = dot_nn(lgd[0], tkr[0])
    for d in range(1, dp):
        term = term + dot_nn(lgd[d], tkr[d])
    for j in range(ep):
        ws[j] = term[j * exp_dev:(j + 1) * exp_dev, :]
    wr[me] = ws[me]
    loop_ep(lambda s_: remote(ws.at[ep_peer(s_)], wr.at[me], s_w.at[s_], r_w.at[me], ep_id(ep_peer(s_))).start())

    def w_arrival(s_):
        src = lax.rem(me + ep - s_, ep)
        remote(ws.at[src], wr.at[src], s_w.at[s_], r_w.at[src], ep_id(src)).wait_recv()

    loop_ep(w_arrival)
    out = lax.fori_loop(1, ep, lambda j, acc: acc + wr[j], wr[0])
    wg_out[...] = out / math.sqrt(token_total)

    loop_ep(lambda s_: idx_copy(s_).wait_send())
    loop_ep(lambda s_: remote(st_ep.at[me], st_ep.at[me], s_se.at[s_], r_se.at[me], ep_id(ep_peer(s_))).wait_send())
    loop_ep(lambda s_: reply(ep_peer(s_)).wait_send())
    loop_ep(lambda s_: remote(ws.at[ep_peer(s_)], wr.at[me], s_w.at[s_], r_w.at[me], ep_id(ep_peer(s_))).wait_send())
    for s in range(1, dp):
        sd_copy(s).wait_send()
        tk_copy(s).wait_send()
        lg_copy(s).wait_send()

    def drain(q, carry):
        for c in range(chunks):
            right = jnp.logical_and(q <= pos, pos < last)
            left = jnp.logical_and(q >= pos, pos > 0)
            used = q >= 0
            if c in swapped:
                right = jnp.logical_and(right, jnp.logical_or(q < pos, pos < last - 1))
                left = jnp.logical_and(left, jnp.logical_or(q > pos, pos > 1))
                used = jnp.logical_not(jnp.logical_and(at_end, q == near))

            @pl.when(used)
            def _():
                leaf(q, c).wait_send()

            @pl.when(right)
            def _():
                to_right(q, c).wait_send()

            @pl.when(left)
            def _():
                to_left(q, c).wait_send()
        return carry

    if len(swapped):
        @pl.when(at_end)
        def _():
            for c in swapped:
                for b in range(2):
                    send_back(b, c).wait_send()
    lax.fori_loop(0, line, drain, 0)


def on_device(tokens, out_grad, indices, expert_rows, router_weight, router_bias, balance_scale):
    tok_dev, width = tokens.shape
    chosen = indices.shape[1]
    experts = router_weight.shape[1]
    exp_dev, cap = expert_rows.shape[1], expert_rows.shape[3]
    ep = lax.axis_size("ep")
    dp = lax.axis_size("dp")
    line = ep // 2
    packed = -(-min(tok_dev, (exp_dev - 1) * cap) // 16) * 16
    widths = tuple(min(CHUNK, width - s) for s in range(0, width, CHUNK))
    chunks = len(widths)
    cfg = (ep, dp, tok_dev, chosen, experts, exp_dev, cap, packed, widths, tok_dev * ep * dp)
    part = width // dp
    rows_t = jnp.transpose(expert_rows[0], (0, 2, 1, 3)).reshape(exp_dev, cap * ep, width)
    vmem = pl.BlockSpec(memory_space=pltpu.VMEM)
    hbm = pl.BlockSpec(memory_space=pl.ANY)
    smem = pl.BlockSpec(memory_space=pltpu.SMEM)
    dma = pltpu.SemaphoreType.DMA
    scratch = [pltpu.VMEM((line, tok_dev, w), BF16) for w in widths]
    scratch += [pltpu.VMEM((line, packed, w), BF16) for w in widths]
    scratch += [pltpu.VMEM((line, packed, w), BF16) for w in widths]
    scratch += [pltpu.VMEM((ep, -(-exp_dev * cap // 16) * 16, w), BF16) for w in widths]
    scratch += [pltpu.VMEM((2, -(-exp_dev * cap // 16) * 16, w), BF16) for w in widths]
    scratch += [
        pltpu.VMEM((exp_dev, cap * ep, width), BF16),
        pltpu.VMEM((exp_dev, ep * (-(-cap // 8) * 8), widths[0]), F32),
        pltpu.VMEM((2, 8, tok_dev), F32),
        pltpu.VMEM((2, 8, tok_dev), F32),
        dma((2, chunks)), dma((2, chunks)),
        pltpu.VMEM((ep, chosen, tok_dev), jnp.int32),
        pltpu.VMEM((line, packed, tok_dev), BF16),
        pltpu.VMEM((line, packed, tok_dev), BF16),
        pltpu.VMEM((line, 8, tok_dev), F32),
        pltpu.VMEM((line, 8, packed), F32),
        pltpu.VMEM((line, 8, tok_dev), F32),
        pltpu.VMEM((line, 8, packed), F32),
        pltpu.VMEM((ep, 8, tok_dev), F32),
        pltpu.VMEM((ep, 8, tok_dev), F32),
        pltpu.VMEM((dp, tok_dev, part), BF16),
        pltpu.VMEM((dp, tok_dev, part), BF16),
        pltpu.VMEM((experts, tok_dev), F32),
        pltpu.VMEM((experts, tok_dev), F32),
        pltpu.VMEM((experts, tok_dev), F32),
        pltpu.VMEM((dp, 8, experts), F32),
        pltpu.VMEM((ep, 8, experts), F32),
        pltpu.VMEM((dp, experts, tok_dev), BF16),
        pltpu.VMEM((ep, exp_dev, part), F32),
        pltpu.VMEM((ep, exp_dev, part), F32),
        dma, dma((chunks,)), dma((ep,)), dma((ep,)),
        dma((line, chunks)), dma((line, chunks)), dma((line, chunks)),
        dma((line, chunks)), dma((line, chunks)), dma((ep,)), dma((ep,)),
        dma((dp,)), dma((dp,)), dma((dp,)), dma((dp,)), dma((ep,)), dma((ep,)),
        dma((dp,)), dma((dp,)), dma((ep,)), dma((ep,)),
    ]
    lg, wg, loss = pl.pallas_call(
        functools.partial(kernel, cfg),
        name="router_backward",
        out_shape=(
            jax.ShapeDtypeStruct((experts, tok_dev), BF16),
            jax.ShapeDtypeStruct((exp_dev, part), F32),
            jax.ShapeDtypeStruct((1, 1), F32),
        ),
        in_specs=[vmem, hbm, hbm, vmem, vmem, vmem, smem],
        out_specs=(vmem, vmem, vmem),
        scratch_shapes=scratch,
        compiler_params=pltpu.CompilerParams(
            collective_id=0, has_side_effects=True, vmem_limit_bytes=56 * 1024 * 1024
        ),
    )(indices.T, out_grad, rows_t, tokens, router_weight.T, router_bias.reshape(1, experts), balance_scale)
    token_grad = lax.dot_general(
        lg, router_weight, (((0,), (1,)), ((), ())), preferred_element_type=F32
    ).astype(BF16)
    return (token_grad, wg.T, loss.reshape(1))


def solution(mesh):
    placed = (
        P(("ep", "dp"), None),
        P(("ep", "dp"), None),
        P(("ep", "dp"), None),
        P("dp", "ep", None, None, None),
        P(),
        P(),
        P(),
    )
    return jax.shard_map(
        on_device,
        mesh=mesh,
        in_specs=placed,
        out_specs=(P(("ep", "dp"), None), P("dp", "ep"), P()),
        check_vma=False,
    )
```

profile of v0, /device:TPU:0, one launch (start us, length us, event | category | flops | bytes accessed | tf_op | source)
XLA Modules:
  0.0 101.8 jit_solution(1201164732426557908)
XLA Ops:
  1.3 0.0 copy-start
  1.3 95.9 %router_backward.1 = (bf16[32,192]{1,0:T(8,128)(2,1)}, f32[4,720]{1,0:T(4,128)}, f32[1,1]{1,0:T(1,128)}) custom-call(s32[4,192]{1,0:T(4,128)} %bitcast.15, bf16[192,2880]{1,0:T(8,128)(2,1)} %refs_1_.1, bf16[4,288,2880]{2,1,0:T(8,128)(2,1)} %bitcast.12, bf16[192,2880]{1,0:T(8,128)(2,1)} %refs_3_.1, bf16[32,2880]{1,0:T(8,128)(2,1)} %bitcast.13, ...), custom_call_target="tpu_custom_call" | custom-call | tf_op jit(solution)/shard_map/router_backward/pallas_call | solution.py:523
  97.2 0.0 copy-start.1
  97.2 0.0 copy-done
  97.2 2.2 %convolution_convert_fusion = bf16[192,2880]{1,0:T(8,128)(2,1)} fusion(bf16[32,192]{1,0:T(8,128)(2,1)} %get-tuple-element.6, bf16[2880,32]{0,1:T(8,128)(2,1)S(1)} %copy-done), kind=kOutput, calls=%fused_computation | convolution fusion | flops 35942400 | bytes 1302528 | tf_op jit(solution)/shard_map/dot_general | solution.py:538
  99.4 0.0 copy-done.1
  99.4 0.6 copy.13
Async XLA Ops:
  1.3 95.9 %copy-start = (bf16[2880,32]{0,1:T(8,128)(2,1)S(1)}, bf16[2880,32]{0,1:T(8,128)(2,1)}, u32[]{:S(2)}) copy-start(bf16[2880,32]{0,1:T(8,128)(2,1)} %param.11) | copy-start | bytes 552964
  97.2 2.2 %copy-start.1 = (f32[4,720]{1,0:T(4,128)S(1)}, f32[4,720]{1,0:T(4,128)}, u32[]{:S(2)}) copy-start(f32[4,720]{1,0:T(4,128)} %get-tuple-element.7) | copy-start | bytes 34564
where the time goes:
time: 102 us
  Pallas kernels  95.9 us (94%)
  between operations  3.06 us (3%)
  matrix products  2.2 us (2%)
    pallas_call x1, Pallas kernels, on_device(): pl.pallas_call(functools.partial(kernel, cfg), name='router_backward', ou...  95.9 us
    dot_general x1, matrix products, on_device(): lax.dot_general(lg, router_weight, (((0,), (1,)), ((), ())), preferred_el...  2.2 us

commit v1 on v0

v1 whole, which is shorter than its diff:
```python
import functools
import math

import jax
import jax.numpy as jnp
from jax import lax
from jax.experimental import pallas as pl
from jax.experimental.pallas import tpu as pltpu
from jax.sharding import PartitionSpec as P

MESH = pl.DeviceIdType.MESH
F32 = jnp.float32
BF16 = jnp.bfloat16
CHUNK = 768
LAG = 4


def dot_nt(x, y, precision=None):
    return lax.dot_general(
        x, y, (((1,), (1,)), ((), ())), preferred_element_type=F32, precision=precision
    )


def dot_nn(x, y, precision=None):
    return lax.dot_general(
        x, y, (((1,), (0,)), ((), ())), preferred_element_type=F32, precision=precision
    )


def kernel(cfg, *refs):
    (ep, dp, tok_dev, chosen, experts, exp_dev, cap, packed, widths, starts, swapped, late, token_total) = cfg
    line = ep // 2
    last = line - 1
    chunks = len(widths)
    every = range(chunks)
    kept = [c for c in every if c not in swapped]
    (idx_in, grad_in, rows_in, tok_in, wt_in, bias_in, scale_in, tg_out, wg_out, loss_out) = refs[:10]
    refs = refs[10:]
    hop = refs[5 * chunks:6 * chunks]
    hop_n = refs[6 * chunks:7 * chunks]
    back_n = refs[7 * chunks:8 * chunks]
    xb = refs[:chunks]
    lsend = refs[chunks:2 * chunks]
    lrecv = refs[2 * chunks:3 * chunks]
    rows_v = refs[3 * chunks:4 * chunks]
    back = refs[4 * chunks:5 * chunks]
    (tok_v, wt_v, bias_v, scale_v, s_in, loss_v, wg_v, s_out,
     rows_raw, piled, tgt_r, acc_r, rst_r, rbuf_r, s_back, r_back, r_hop, s_near, r_hop_n, r_back_n, s_rr, r_rr, tgt_n, acc_n, tg_v,
     idx_all, pin, pout, tgt_x, tgt_p, acc_x, acc_p, rst, rbuf, tks, tkr, logit_v, prob_v,
     named_v, st_dp, st_m, st_z, lgd, ws, wr,
     s_rows, s_own, s_idx, r_idx, s_right, s_left, r_x, s_leaf, r_leaf, s_rep, r_rep,
     s_tk, r_tk, s_sd, r_sd, s_st, r_st, s_lg, r_lg, s_w, r_w) = refs[8 * chunks:]
    me = lax.axis_index("ep")
    md = lax.axis_index("dp")
    pos = me // 2
    side = lax.rem(me, 2)
    mate = pos * 2 + 1 - side
    at_end = jnp.logical_or(pos == 0, pos == last)
    near_end = jnp.logical_or(pos == 1, pos == last - 1)
    end = jnp.where(pos * 2 < line, 0, last)
    near = jnp.where(pos * 2 < line, 1, last - 1)
    far = last - end

    def ep_id(other):
        return (other, md)

    def remote(src, dst, s, r, dev):
        return pltpu.make_async_remote_copy(
            src_ref=src, dst_ref=dst, send_sem=s, recv_sem=r, device_id=dev, device_id_type=MESH
        )

    def ep_peer(s):
        return lax.rem(me + s, ep)

    def dp_peer(s):
        return lax.rem(md + s, dp)

    barrier = pltpu.get_barrier_semaphore()

    def greet(dev):
        pl.semaphore_signal(barrier, inc=1, device_id=dev, device_id_type=MESH)

    @pl.when(pos < last)
    def _():
        greet(ep_id(me + 2))

    @pl.when(pos > 0)
    def _():
        greet(ep_id(me - 2))

    greet(ep_id(mate))
    for s in range(1, dp):
        greet((me, dp_peer(s)))

    idx_here = pltpu.make_async_copy(idx_in, idx_all.at[me], s_in.at[0])
    own = [
        pltpu.make_async_copy(grad_in.at[:, pl.ds(starts[c], widths[c])], xb[c].at[pos], s_own.at[c])
        for c in every
    ]
    rows_copy = pltpu.make_async_copy(rows_in, rows_raw, s_rows)
    small = [
        pltpu.make_async_copy(tok_in, tok_v, s_in.at[1]),
        pltpu.make_async_copy(wt_in, wt_v, s_in.at[2]),
        pltpu.make_async_copy(bias_in, bias_v, s_in.at[3]),
        pltpu.make_async_copy(scale_in, scale_v, s_in.at[4]),
    ]
    idx_here.start()
    for copy in own:
        copy.start()
    rows_copy.start()
    for copy in small:
        copy.start()
    pl.semaphore_wait(
        barrier, dp + (pos < last).astype(jnp.int32) + (pos > 0).astype(jnp.int32)
    )

    def idx_copy(q, way, dev):
        at = q * 2 + side
        return remote(idx_all.at[at], idx_all.at[at], s_idx.at[way], r_idx.at[at], ep_id(dev))

    def idx_right(q):
        return idx_copy(q, 0, me + 2)

    def idx_left(q):
        return idx_copy(q, 1, me - 2)

    def idx_mate(q):
        return idx_copy(q, 2, mate)

    def idx_from_mate(q):
        at = q * 2 + 1 - side
        return remote(idx_all.at[at], idx_all.at[at], s_idx.at[2], r_idx.at[at], ep_id(mate))

    def loop_ep(fn):
        def body(s, carry):
            fn(s)
            return carry
        lax.fori_loop(1, ep, body, 0)

    def to_right(q, c):
        return remote(xb[c].at[q], xb[c].at[q], s_right.at[c], r_x.at[q, c], ep_id(me + 2))

    def to_left(q, c):
        return remote(xb[c].at[q], xb[c].at[q], s_left.at[c], r_x.at[q, c], ep_id(me - 2))

    def leaf(q, c):
        return remote(lsend[c].at[q], lrecv[c].at[q], s_leaf.at[c], r_leaf.at[q, c], ep_id(mate))

    def hop_rows(c):
        return remote(rows_v[c].at[far * 2 + 1 - side], hop[c], s_back.at[c], r_hop.at[c], ep_id(mate))

    def send_back(b, c):
        src = rows_v[c].at[far * 2 + side] if b == 0 else hop[c]
        at = side if b == 0 else 1 - side
        return remote(src, back[c].at[at], s_back.at[c], r_back.at[c], ep_id(near * 2 + side))

    def back_arrival(c):
        return remote(back[c], back[c], s_back.at[c], r_back.at[c], ep_id(end * 2 + side))

    def hop_near(c):
        return remote(rows_v[c].at[near * 2 + 1 - side], hop_n[c], s_near.at[c], r_hop_n.at[c], ep_id(mate))

    def send_near(c):
        return remote(hop_n[c], back_n[c], s_near.at[c], r_back_n.at[c], ep_id(near * 2 + side))

    def near_arrival(c):
        return remote(back_n[c], back_n[c], s_near.at[c], r_back_n.at[c], ep_id(end * 2 + side))

    def back_reply():
        return remote(rst_r, rbuf_r, s_rr, r_rr, ep_id(far * 2 + side))

    def back_reply_arrival():
        return remote(rst_r, rbuf_r, s_rr, r_rr, ep_id((last - near) * 2 + side))

    def reply(j):
        return remote(rst.at[j], rbuf.at[me], s_rep, r_rep, ep_id(j))

    def st_copy(q, way, dev):
        return remote(st_z.at[q], st_z.at[q], s_st.at[way], r_st.at[q], ep_id(dev))

    def st_right(q):
        return st_copy(q, 0, me + 2)

    def st_left(q):
        return st_copy(q, 1, me - 2)

    def st_mate(at):
        return remote(st_m.at[at], st_m.at[at], s_st.at[2], r_st.at[line], ep_id(mate))

    for copy in own:
        copy.wait()
    idx_here.wait()

    @pl.when(pos < last)
    def _():
        idx_right(pos).start()

    @pl.when(pos > 0)
    def _():
        idx_left(pos).start()

    idx_mate(pos).start()
    for c in every:
        @pl.when(pos < last - (c in late))
        def _():
            to_right(pos, c).start()

        @pl.when(pos > 0 + (c in late))
        def _():
            to_left(pos, c).start()

    expert_row = lax.broadcasted_iota(jnp.int32, (experts, tok_dev), 0)
    eye_r = lax.broadcasted_iota(jnp.int32, (experts, experts), 0)
    eye_c = lax.broadcasted_iota(jnp.int32, (experts, experts), 1)
    t_from = lax.broadcasted_iota(jnp.int32, (tok_dev, tok_dev), 0)
    t_to = lax.broadcasted_iota(jnp.int32, (tok_dev, tok_dev), 1)
    upper = jnp.where(t_from < t_to, 1.0, 0.0).astype(BF16)
    row8 = lax.broadcasted_iota(jnp.int32, (8, tok_dev), 0)
    slot_p = lax.broadcasted_iota(jnp.int32, (packed, tok_dev), 0).astype(F32)

    def upright(line_of):
        return jnp.sum(jnp.where(eye_r == eye_c, line_of, 0.0), axis=1, keepdims=True)

    def plan(table, group):
        who = jnp.where(row8 < exp_dev, group * exp_dev + row8, -2)
        hit = jnp.zeros((8, tok_dev), F32)
        for k in range(chosen):
            hit = hit + jnp.where(table[k:k + 1, :] == who, 1.0, 0.0)
        need = jnp.max(hit, axis=0, keepdims=True)
        stack = jnp.where(row8 == exp_dev, need, hit)
        before = dot_nn(stack.astype(BF16), upper)
        place = jnp.where(need > 0.5, before[exp_dev:exp_dev + 1, :], -1.0)
        target = jnp.where(hit > 0.5, before, -1.0)
        pack = jnp.where(slot_p == place, 1.0, 0.0).astype(BF16)
        return target, pack

    def plan_block(q):
        table = idx_all[q * 2 + side]
        _, pack = plan(table, mate)
        pout[q] = pack
        target, _ = plan(table, me)
        tgt_x[q] = target
        acc_x[q] = jnp.zeros((8, tok_dev), F32)

    def plan_leaf(q):
        target, pack = plan(idx_all[q * 2 + 1 - side], me)
        pin[q] = pack
        tgt_p[q] = dot_nt((target + 1.0).astype(BF16), pack) - 1.0
        acc_p[q] = jnp.zeros((8, packed), F32)

    def plan_back():
        for b in range(2):
            tgt_r[b], _ = plan(idx_all[far * 2 + side], end * 2 + b)
            acc_r[b] = jnp.zeros((8, tok_dev), F32)
        tgt_n[...], _ = plan(idx_all[me], end * 2 + 1 - side)
        acc_n[...] = jnp.zeros((8, tok_dev), F32)

    deep = piled.shape[1] // ep
    slot_r = lax.broadcasted_iota(jnp.int32, (deep, cap * ep), 0)
    lies = lax.broadcasted_iota(jnp.int32, (deep, cap * ep), 1)
    spare = rows_v[0].shape[1] - exp_dev * cap

    def sort_rows(c):
        w = widths[c]
        order = jnp.concatenate(
            [jnp.where(jnp.logical_and(lies == slot_r * ep + j, slot_r < cap), 1.0, 0.0) for j in range(ep)], axis=0
        ).astype(BF16)
        for e in range(exp_dev):
            piled[e, :, 0:w] = dot_nn(order, rows_raw[e, :, starts[c]:starts[c] + w])

        def put(j, carry):
            at = pl.ds(pl.multiple_of(j * deep, 8), deep)
            pieces = [piled[e, at, 0:w][0:cap, :] for e in range(exp_dev)]
            if spare:
                pieces.append(jnp.zeros((spare, w), F32))
            rows_v[c][j] = jnp.concatenate(pieces, axis=0).astype(BF16)
            return carry

        lax.fori_loop(0, ep, put, 0)

    def gathered(table, block, target, count):
        height = table.shape[0]
        slot = lax.broadcasted_iota(jnp.int32, (height, count), 0).astype(F32)
        row = lax.broadcasted_iota(jnp.int32, (8, count), 0)
        dots = dot_nt(table, block)
        out = jnp.zeros((8, count), F32)
        for e in range(exp_dev):
            want = jnp.where(target[e:e + 1, :] >= 0.0, target[e:e + 1, :] + e * cap, -1.0)
            one = jnp.sum(jnp.where(slot == want, dots, 0.0), axis=0, keepdims=True)
            out = jnp.where(row == e, one, out)
        return out

    def give_leaf(q, c):
        lsend[c][q] = dot_nn(pout[q], xb[c][q]).astype(BF16)
        leaf(q, c).start()

    def use_block(q, c):
        acc_x[q] += gathered(rows_v[c][q * 2 + side], xb[c][q], tgt_x[q], tok_dev)

    def use_leaf(q, c):
        leaf(q, c).wait_recv()
        acc_p[q] += gathered(rows_v[c][q * 2 + 1 - side], lrecv[c][q], tgt_p[q], packed)

    def answer(j, value):
        rst[j] = value
        reply(j).start()

    def done_block(q):
        answer(q * 2 + side, acc_x[q])

    def done_leaf(q):
        answer(q * 2 + 1 - side, dot_nn(acc_p[q], pin[q].astype(F32), lax.Precision.HIGHEST))

    def meets(s, c, tail):
        left, right = pos - s >= 0, pos + s < line
        if s == last and c in swapped:
            return ()
        if s == 1 and c in late:
            inner = at_end if tail else jnp.logical_not(at_end)
            left, right = jnp.logical_and(left, inner), jnp.logical_and(right, inner)
        return ((pos - s, left, True), (pos + s, right, False))

    def closes(s, c, tail, finish, q):
        if s == 1 and len(late) and finish is done_block:
            if tail:
                if c == late[-1]:
                    finish(q)
            elif c == chunks - 1:
                @pl.when(jnp.logical_not(at_end))
                def _():
                    finish(q)
        elif c == (kept[-1] if s == last else chunks - 1):
            finish(q)

    def learn(s):
        for q, ok, rightward in ((pos - s, pos - s >= 0, True), (pos + s, pos + s < line, False)):
            @pl.when(ok)
            def _(q=q, rightward=rightward):
                step = idx_right if rightward else idx_left
                step(q).wait_recv()

                @pl.when(pos < last if rightward else pos > 0)
                def _():
                    step(q).start()
                    if s == last - 1 and len(swapped):
                        plan_back()

                idx_mate(q).start()
                plan_block(q)

    def learn_leaf(s):
        for q, ok in ((pos - s, pos - s >= 0), (pos + s, pos + s < line))[:1 if s == 0 else 2]:
            @pl.when(ok)
            def _(q=q):
                idx_from_mate(q).wait_recv()
                plan_leaf(q)

    def arrive(s, c, tail=False):
        for q, ok, rightward in meets(s, c, tail):
            @pl.when(ok)
            def _(q=q, rightward=rightward):
                step = to_right if rightward else to_left
                step(q, c).wait_recv()

                @pl.when(pos < last if rightward else pos > 0)
                def _():
                    if not (s == last - 1 and c in swapped):
                        step(q, c).start()
                    if s == last - 1 and c == kept[-1]:
                        for n in late:
                            step(pos, n).start()

                if not tail:
                    give_leaf(q, c)

    def use(s, c, tail=False):
        for q, ok, rightward in meets(s, c, tail):
            @pl.when(ok)
            def _(q=q, rightward=rightward):
                use_block(q, c)
                closes(s, c, tail, done_block, q)
                if s == last - 1 and c in swapped:
                    @pl.when(pos < last if rightward else pos > 0)
                    def _():
                        back_arrival(c).wait_recv()
                        for b in range(2):
                            acc_r[b] += gathered(back[c][b], xb[c][q], tgt_r[b], tok_dev)
                        if c == swapped[-1]:
                            rst_r[...] = acc_r[...]
                            back_reply().start()
                            for n in late:
                                near_arrival(n).wait_recv()
                                acc_n[...] += gathered(back_n[n][...], xb[n][pos], tgt_n[...], tok_dev)

    def take(s, c):
        if s == 0:
            use_leaf(pos, c)
            if c == chunks - 1:
                done_leaf(pos)
            return
        for q, ok, _ in meets(s, c, False):
            @pl.when(ok)
            def _(q=q):
                use_leaf(q, c)
                closes(s, c, False, done_leaf, q)

    def settle(s, c):
        if c == 0:
            learn_leaf(s)
        take(s, c)

    def pass_rows(c):
        @pl.when(at_end)
        def _():
            if c in swapped:
                hop_rows(c).wait_recv()
                send_back(1, c).start()
            if c in late:
                hop_near(c).wait_recv()
                send_near(c).start()

    def sort_step(c):
        sort_rows(c)
        if c in swapped or c in late:
            @pl.when(at_end)
            def _():
                if c in swapped:
                    hop_rows(c).start()
                    send_back(0, c).start()
                if c in late:
                    hop_near(c).start()
        use_block(pos, c)
        if c == chunks - 1:
            rbuf[me] = acc_x[pos]

    part = tok_in.shape[1] // dp

    def tk_copy(s):
        return remote(tks.at[dp_peer(s)], tkr.at[md], s_tk, r_tk, (me, dp_peer(s)))

    def tk_all():
        return remote(tks.at[pl.ds(0, dp - 1)], tkr.at[pl.ds(0, dp - 1)], s_tk, r_tk, (me, dp_peer(1)))

    def sd_copy(s):
        return remote(st_dp.at[md], st_dp.at[md], s_sd, r_sd, (me, dp_peer(s)))

    def sd_all():
        return remote(st_dp.at[pl.ds(0, dp - 1)], st_dp.at[pl.ds(0, dp - 1)], s_sd, r_sd, (me, dp_peer(1)))

    def route():
        for copy in small:
            copy.wait()
        idx = idx_all[me]
        named = jnp.zeros((experts, tok_dev), F32)
        for k in range(chosen):
            named = named + jnp.where(idx[k:k + 1, :] == expert_row, 1.0, 0.0)
        logits = dot_nt(wt_v[...], tok_v[...]) + upright(bias_v[...])
        top = jnp.max(logits, axis=0, keepdims=True)
        power = jnp.exp(logits - top)
        prob = power / jnp.sum(power, axis=0, keepdims=True)
        logit_v[...] = logits
        prob_v[...] = prob
        named_v[...] = named
        ones = jnp.ones((8, tok_dev), F32)
        count_row = dot_nt(ones, named, lax.Precision.HIGHEST)
        prob_row = dot_nt(ones, prob, lax.Precision.HIGHEST)
        stat_row = lax.broadcasted_iota(jnp.int32, (8, experts), 0)
        st_dp[md] = jnp.where(stat_row == 0, count_row, prob_row)
        for s in range(1, dp):
            sd_copy(s).start()

    def share_tokens():
        for d in range(dp):
            tks[d] = tok_v[:, d * part:(d + 1) * part]
        for s in range(1, dp):
            tk_copy(s).start()
        tkr[md] = tks[md]

    def pair_stats():
        sd_all().wait_recv()
        total = st_dp[0]
        for d in range(1, dp):
            total = total + st_dp[d]
        st_m[side] = total
        st_mate(side).start()

    def share_stats():
        st_mate(1 - side).wait_recv()
        st_z[pos] = st_m[0] + st_m[1]

        @pl.when(pos < last)
        def _():
            st_right(pos).start()

        @pl.when(pos > 0)
        def _():
            st_left(pos).start()

    def pass_stats(s):
        for q, ok, rightward in ((pos - s, pos - s >= 0, True), (pos + s, pos + s < line, False)):
            @pl.when(ok)
            def _(q=q, rightward=rightward):
                step = st_right if rightward else st_left
                step(q).wait_recv()

                @pl.when(pos < last if rightward else pos > 0)
                def _():
                    step(q).start()

    plan_block(pos)
    for c in every:
        give_leaf(pos, c)
    rows_copy.wait()
    for c in every:
        if c == max(chunks - 2, 0):
            learn(1)
            arrive(1, 0)
        sort_step(c)
    steps = [(0, c) for c in every] + [(s, c) for s in range(1, line) for c in every]
    taken = 0
    for n, (s, c) in enumerate(steps):
        if s > 0:
            if c == 0:
                if s > 1:
                    learn(s)
            if (s, c) != (1, 0):
                arrive(s, c)
            use(s, c)
            if s == 2 and (c in swapped or c in late):
                pass_rows(c)
            if s == 2 and c == chunks - 1:
                pass_stats(1)
            if (s, c) == (1, 1 if chunks > 1 else 0):
                route()
                share_tokens()
            if (s, c) == (1, max(chunks - 2, 0)):
                pair_stats()
            if (s, c) == ((2, 0) if last > 1 else (1, chunks - 1)):
                share_stats()
            while taken <= n - LAG:
                settle(*steps[taken])
                taken += 1
    for c in late:
        arrive(1, c, True)
        use(1, c, True)
    for step in steps[taken:]:
        settle(*step)
    for s in range(2 if last > 1 else 1, line):
        pass_stats(s)
    stats = st_z[0]
    for q in range(1, line):
        stats = stats + st_z[q]
    share = stats[0:1, :] / (token_total * chosen)
    mean = stats[1:2, :] / token_total
    loss_v[...] = experts * jnp.sum(share * mean, axis=1, keepdims=True)
    loss_copy = pltpu.make_async_copy(loss_v, loss_out, s_out.at[0])
    loss_copy.start()
    push_row = scale_v[...] * experts * share
    push = upright(push_row)
    prob = prob_v[...]
    spread = prob * (push - jnp.sum(prob * push, axis=0, keepdims=True))
    named = named_v[...]
    logits = logit_v[...]
    high = jnp.max(jnp.where(named > 0.5, logits, -jnp.inf), axis=0, keepdims=True)
    mix = jnp.where(named > 0.5, jnp.exp(jnp.minimum(logits - high, 0.0)), 0.0)
    mix = mix / jnp.sum(mix, axis=0, keepdims=True)

    remote(rst.at[pl.ds(0, ep - 1)], rbuf.at[pl.ds(0, ep - 1)], s_rep, r_rep, ep_id(mate)).wait_recv()
    if len(swapped):
        @pl.when(at_end)
        def _():
            back_reply_arrival().wait_recv()
            for b in range(2):
                rbuf[far * 2 + b] += rbuf_r[b]

        @pl.when(near_end)
        def _():
            rbuf[end * 2 + 1 - side] += acc_n[...]
    dots = jnp.concatenate([rbuf[j, 0:exp_dev, :] for j in range(ep)], axis=0)
    sel = mix * (dots - jnp.sum(mix * dots, axis=0, keepdims=True))
    grad = (spread + sel).astype(BF16)
    lgd[md] = grad

    def lg_copy(s):
        return remote(lgd.at[md], lgd.at[md], s_lg, r_lg, (me, dp_peer(s)))

    def lg_all():
        return remote(lgd.at[pl.ds(0, dp - 1)], lgd.at[pl.ds(0, dp - 1)], s_lg, r_lg, (me, dp_peer(1)))

    for s in range(1, dp):
        lg_copy(s).start()
    for c in every:
        at = slice(starts[c], starts[c] + widths[c])
        tg_v[:, at] = lax.dot_general(
            grad, wt_v[:, at], (((0,), (0,)), ((), ())), preferred_element_type=F32
        ).astype(BF16)
    tg_store = pltpu.make_async_copy(tg_v, tg_out, s_out.at[1])
    tg_store.start()
    tk_all().wait_recv()
    lg_all().wait_recv()
    term = dot_nn(lgd[0], tkr[0])
    for d in range(1, dp):
        term = term + dot_nn(lgd[d], tkr[d])
    for j in range(ep):
        ws[j] = term[j * exp_dev:(j + 1) * exp_dev, :]
    wr[me] = ws[me]

    def w_copy(s_):
        return remote(ws.at[ep_peer(s_)], wr.at[me], s_w, r_w, ep_id(ep_peer(s_)))

    def w_all():
        return remote(ws.at[pl.ds(0, ep - 1)], wr.at[pl.ds(0, ep - 1)], s_w, r_w, ep_id(mate))

    loop_ep(lambda s_: w_copy(s_).start())

    def sent(ref, sem, count):
        for n in range(1, line + 1):
            @pl.when(count == n)
            def _(n=n):
                piece = ref.at[pl.ds(0, n)]
                remote(piece, piece, sem, sem, ep_id(mate)).wait_send()

    ups = jnp.where(pos < last, pos + 1, 0)
    downs = jnp.where(pos > 0, line - pos, 0)
    for buf, sem in ((idx_all, s_idx), (st_z, s_st)):
        sent(buf, sem.at[0], ups)
        sent(buf, sem.at[1], downs)
    sent(idx_all, s_idx.at[2], line)
    st_mate(side).wait_send()
    for c in every:
        short = 1 if c in swapped else 0
        sent(xb[c], s_right.at[c], ups - jnp.where(pos == last - 1, short, 0))
        sent(xb[c], s_left.at[c], downs - jnp.where(pos == 1, short, 0))
        skipped = short + (1 if c in late else 0)
        sent(lsend[c], s_leaf.at[c], line - jnp.where(at_end, skipped, 0))
    if len(swapped):
        @pl.when(at_end)
        def _():
            for c in swapped:
                piece = rows_v[c].at[pl.ds(0, 3)]
                remote(piece, piece, s_back.at[c], s_back.at[c], ep_id(mate)).wait_send()
            for c in late:
                piece = rows_v[c].at[pl.ds(0, 2)]
                remote(piece, piece, s_near.at[c], s_near.at[c], ep_id(mate)).wait_send()

        @pl.when(near_end)
        def _():
            back_reply().wait_send()
    remote(rst.at[pl.ds(0, ep - 1)], rbuf.at[pl.ds(0, ep - 1)], s_rep, r_rep, ep_id(mate)).wait_send()
    sd_all().wait_send()
    tk_all().wait_send()
    lg_all().wait_send()
    loss_copy.wait()
    tg_store.wait()
    w_all().wait_recv()
    out = lax.fori_loop(1, ep, lambda j, acc: acc + wr[j], wr[0])
    wg_v[...] = out / math.sqrt(token_total)
    wg_copy = pltpu.make_async_copy(wg_v, wg_out, s_out.at[2])
    wg_copy.start()
    w_all().wait_send()
    wg_copy.wait()


def cut(width):
    if width <= 3 * CHUNK + CHUNK // 2 or width > 4 * CHUNK:
        widths = tuple(min(CHUNK, width - s) for s in range(0, width, CHUNK))
        return widths, tuple(sum(widths[:c]) for c in range(len(widths))), (), ()
    half = CHUNK // 2
    rest = width - 3 * CHUNK - half
    return (CHUNK, rest, half, CHUNK, CHUNK), (0, width - rest, CHUNK, CHUNK + half, 2 * CHUNK + half), (2, 3, 4), (2, 1)


def on_device(tokens, out_grad, indices, expert_rows, router_weight, router_bias, balance_scale):
    tok_dev, width = tokens.shape
    chosen = indices.shape[1]
    experts = router_weight.shape[1]
    exp_dev, cap = expert_rows.shape[1], expert_rows.shape[3]
    ep = lax.axis_size("ep")
    dp = lax.axis_size("dp")
    line = ep // 2
    packed = -(-min(tok_dev, (exp_dev - 1) * cap) // 16) * 16
    widths, starts, swapped, late = cut(width)
    chunks = len(widths)
    if line < 4:
        swapped, late = (), ()
    cfg = (ep, dp, tok_dev, chosen, experts, exp_dev, cap, packed, widths, starts, swapped, late, tok_dev * ep * dp)
    part = width // dp
    rows_t = jnp.transpose(expert_rows[0], (0, 2, 1, 3)).reshape(exp_dev, cap * ep, width)
    hbm = pl.BlockSpec(memory_space=pl.ANY)
    dma = pltpu.SemaphoreType.DMA
    scratch = [pltpu.VMEM((line, tok_dev, w), BF16) for w in widths]
    scratch += [pltpu.VMEM((line, packed, w), BF16) for w in widths]
    scratch += [pltpu.VMEM((line, packed, w), BF16) for w in widths]
    scratch += [pltpu.VMEM((ep, -(-exp_dev * cap // 16) * 16, w), BF16) for w in widths]
    scratch += [pltpu.VMEM((2, -(-exp_dev * cap // 16) * 16, w), BF16) for w in widths]
    scratch += [pltpu.VMEM((-(-exp_dev * cap // 16) * 16, w), BF16) for w in widths]
    scratch += [pltpu.VMEM((-(-exp_dev * cap // 16) * 16, w), BF16) for w in widths]
    scratch += [pltpu.VMEM((-(-exp_dev * cap // 16) * 16, w), BF16) for w in widths]
    scratch += [
        pltpu.VMEM((tok_dev, width), BF16),
        pltpu.VMEM((experts, width), BF16),
        pltpu.VMEM((1, experts), F32),
        pltpu.VMEM((1, 1), F32),
        dma((5,)),
        pltpu.VMEM((1, 1), F32),
        pltpu.VMEM((exp_dev, part), F32),
        dma((3,)),
        pltpu.VMEM((exp_dev, cap * ep, width), BF16),
        pltpu.VMEM((exp_dev, ep * (-(-cap // 8) * 8), max(widths)), F32),
        pltpu.VMEM((2, 8, tok_dev), F32),
        pltpu.VMEM((2, 8, tok_dev), F32),
        pltpu.VMEM((2, 8, tok_dev), F32),
        pltpu.VMEM((2, 8, tok_dev), F32),
        dma((chunks,)), dma((chunks,)), dma((chunks,)), dma((chunks,)), dma((chunks,)), dma((chunks,)), dma, dma,
        pltpu.VMEM((8, tok_dev), F32),
        pltpu.VMEM((8, tok_dev), F32),
        pltpu.VMEM((tok_dev, width), BF16),
        pltpu.VMEM((ep, chosen, tok_dev), jnp.int32),
        pltpu.VMEM((line, packed, tok_dev), BF16),
        pltpu.VMEM((line, packed, tok_dev), BF16),
        pltpu.VMEM((line, 8, tok_dev), F32),
        pltpu.VMEM((line, 8, packed), F32),
        pltpu.VMEM((line, 8, tok_dev), F32),
        pltpu.VMEM((line, 8, packed), F32),
        pltpu.VMEM((ep, 8, tok_dev), F32),
        pltpu.VMEM((ep, 8, tok_dev), F32),
        pltpu.VMEM((dp, tok_dev, part), BF16),
        pltpu.VMEM((dp, tok_dev, part), BF16),
        pltpu.VMEM((experts, tok_dev), F32),
        pltpu.VMEM((experts, tok_dev), F32),
        pltpu.VMEM((experts, tok_dev), F32),
        pltpu.VMEM((dp, 8, experts), F32),
        pltpu.VMEM((2, 8, experts), F32),
        pltpu.VMEM((line, 8, experts), F32),
        pltpu.VMEM((dp, experts, tok_dev), BF16),
        pltpu.VMEM((ep, exp_dev, part), F32),
        pltpu.VMEM((ep, exp_dev, part), F32),
        dma, dma((chunks,)), dma((3,)), dma((ep,)),
        dma((chunks,)), dma((chunks,)), dma((line, chunks)),
        dma((chunks,)), dma((line, chunks)), dma, dma,
        dma, dma, dma, dma, dma((3,)), dma((line + 1,)),
        dma, dma, dma, dma,
    ]
    token_grad, wg, loss = pl.pallas_call(
        functools.partial(kernel, cfg),
        name="router_backward",
        out_shape=(
            jax.ShapeDtypeStruct((tok_dev, width), BF16),
            jax.ShapeDtypeStruct((exp_dev, part), F32),
            jax.ShapeDtypeStruct((1, 1), F32),
        ),
        in_specs=[hbm] * 7,
        out_specs=(hbm,) * 3,
        scratch_shapes=scratch,
        compiler_params=pltpu.CompilerParams(
            collective_id=0, has_side_effects=True, vmem_limit_bytes=56 * 1024 * 1024
        ),
    )(indices.T, out_grad, rows_t, tokens, router_weight.T, router_bias.reshape(1, experts), balance_scale.reshape(1, 1))
    return (token_grad, wg.T, loss.reshape(1))


def solution(mesh):
    placed = (
        P(("ep", "dp"), None),
        P(("ep", "dp"), None),
        P(("ep", "dp"), None),
        P("dp", "ep", None, None, None),
        P(),
        P(),
        P(),
    )
    return jax.shard_map(
        on_device,
        mesh=mesh,
        in_specs=placed,
        out_specs=(P(("ep", "dp"), None), P("dp", "ep"), P()),
        check_vma=False,
    )
```

time: 102 us -> 87.2 us (0.85)
  Pallas kernels: 95.9 us -> 81 us
  local copies, waits for them, and re-layouts: 0.61 us -> 2.94 us
  matrix products: 2.2 us -> 0 us
    pallas_call x1, Pallas kernels: 95.9 us -> 81 us  [on_device(): pl.pallas_call(functools.partial(kernel, cfg), name='router_backward', ou...]
    unnamed x5 -> x4, local copies, waits for them, and re-layouts: 0.61 us -> 2.94 us
    dot_general x1 -> x0, matrix products: 2.2 us -> none  [on_device(): lax.dot_general(lg, router_weight, (((0,), (1,)), ((), ())), preferred_el...]
where the time goes in v1:
time: 87.2 us; the launch traced here: 87 us
  Pallas kernels  81 us (93%)
  between operations  3.05 us (3%)
  local copies, waits for them, and re-layouts  2.94 us (3%)
    pallas_call x1, Pallas kernels, on_device(): pl.pallas_call(functools.partial(kernel, cfg), name='router_backward', ou...  81 us
    unnamed x4, local copies, waits for them, and re-layouts  2.94 us

profile of v1, /device:TPU:0, one launch (start us, length us, event | category | flops | bytes accessed | tf_op | source)
XLA Modules:
  0.0 87.0 jit_solution(6238444830202260877)
XLA Ops:
  1.3 81.0 %router_backward.1 = (bf16[192,2880]{1,0:T(8,128)(2,1)}, f32[4,720]{1,0:T(4,128)}, f32[1,1]{1,0:T(1,128)}) custom-call(s32[4,192]{1,0:T(4,128)} %bitcast.15, bf16[192,2880]{1,0:T(8,128)(2,1)} %refs_1_.1, bf16[4,288,2880]{2,1,0:T(8,128)(2,1)} %bitcast.12, bf16[192,2880]{1,0:T(8,128)(2,1)} %refs_3_.1, bf16[32,2880]{1,0:T(8,128)(2,1)} %bitcast.13, ...), custom_call_target="tpu_custom_call" | custom-call | tf_op jit(solution)/shard_map/router_backward/pallas_call | solution.py:744
  82.3 0.0 copy-start
  82.3 2.3 %copy.14 = bf16[192,2880]{1,0:T(8,128)(2,1)} copy(bf16[192,2880]{1,0:T(8,128)(2,1)} %get-tuple-element.12) | data formatting | bytes 2211840
  84.6 0.0 copy-done
  84.6 0.6 copy.15
Async XLA Ops:
  82.3 2.3 %copy-start = (f32[4,720]{1,0:T(4,128)S(1)}, f32[4,720]{1,0:T(4,128)}, u32[]{:S(2)}) copy-start(f32[4,720]{1,0:T(4,128)} %get-tuple-element.7) | copy-start | bytes 34564

commit v2 on v1

--- a/solution.py
+++ b/solution.py
@@ -28,7 +28,7 @@
 
 
 def kernel(cfg, *refs):
-    (ep, dp, tok_dev, chosen, experts, exp_dev, cap, packed, widths, starts, swapped, late, token_total) = cfg
+    (ep, dp, tok_dev, chosen, experts, exp_dev, cap, packed, widths, starts, swapped, late, crossed, direct, held, token_total) = cfg
     line = ep // 2
     last = line - 1
     chunks = len(widths)
@@ -44,12 +44,12 @@
     lrecv = refs[2 * chunks:3 * chunks]
     rows_v = refs[3 * chunks:4 * chunks]
     back = refs[4 * chunks:5 * chunks]
-    (tok_v, wt_v, bias_v, scale_v, s_in, loss_v, wg_v, s_out,
-     rows_raw, piled, tgt_r, acc_r, rst_r, rbuf_r, s_back, r_back, r_hop, s_near, r_hop_n, r_back_n, s_rr, r_rr, tgt_n, acc_n, tg_v,
+    (tok_v, wt_v, bias_v, scale_v, s_in, loss_v, s_out,
+     rows_raw, piled, tgt_r, acc_r, rst_r, rbuf_r, s_back, r_back, r_hop, s_near, r_hop_n, r_back_n, s_rr, r_rr, tgt_n, acc_n,
      idx_all, pin, pout, tgt_x, tgt_p, acc_x, acc_p, rst, rbuf, tks, tkr, logit_v, prob_v,
-     named_v, st_dp, st_m, st_z, lgd, ws, wr,
+     named_v, st_dp, st_ep, lgd, ws, wr,
      s_rows, s_own, s_idx, r_idx, s_right, s_left, r_x, s_leaf, r_leaf, s_rep, r_rep,
-     s_tk, r_tk, s_sd, r_sd, s_st, r_st, s_lg, r_lg, s_w, r_w) = refs[8 * chunks:]
+     s_tk, r_tk, s_sd, r_sd, s_se, r_se, s_ready, s_lg, r_lg, s_w, r_w) = refs[8 * chunks:]
     me = lax.axis_index("ep")
     md = lax.axis_index("dp")
     pos = me // 2
@@ -141,30 +141,35 @@
         return remote(xb[c].at[q], xb[c].at[q], s_right.at[c], r_x.at[q, c], ep_id(me + 2))
 
     def to_left(q, c):
-        return remote(xb[c].at[q], xb[c].at[q], s_left.at[c], r_x.at[q, c], ep_id(me - 2))
+        return remote(xb[c].at[q], xb[c].at[q], s_left.at[c], r_x.at[q - 1, c], ep_id(me - 2))
 
     def leaf(q, c):
         return remote(lsend[c].at[q], lrecv[c].at[q], s_leaf.at[c], r_leaf.at[q, c], ep_id(mate))
 
     def hop_rows(c):
-        return remote(rows_v[c].at[far * 2 + 1 - side], hop[c], s_back.at[c], r_hop.at[c], ep_id(mate))
+        return remote(rows_v[c].at[far * 2 + 1 - side], hop[c], s_back.at[swapped.index(c)], r_hop.at[swapped.index(c)], ep_id(mate))
 
     def send_back(b, c):
         src = rows_v[c].at[far * 2 + side] if b == 0 else hop[c]
         at = side if b == 0 else 1 - side
-        return remote(src, back[c].at[at], s_back.at[c], r_back.at[c], ep_id(near * 2 + side))
+        return remote(src, back[c].at[at], s_back.at[swapped.index(c)], r_back.at[swapped.index(c)], ep_id(near * 2 + side))
 
     def back_arrival(c):
-        return remote(back[c], back[c], s_back.at[c], r_back.at[c], ep_id(end * 2 + side))
+        return remote(back[c], back[c], s_back.at[swapped.index(c)], r_back.at[swapped.index(c)], ep_id(end * 2 + side))
 
     def hop_near(c):
-        return remote(rows_v[c].at[near * 2 + 1 - side], hop_n[c], s_near.at[c], r_hop_n.at[c], ep_id(mate))
+        n = crossed.index(c)
+        return remote(rows_v[c].at[near * 2 + 1 - side], hop_n[c], s_near.at[n], r_hop_n.at[n], ep_id(mate))
 
     def send_near(c):
-        return remote(hop_n[c], back_n[c], s_near.at[c], r_back_n.at[c], ep_id(near * 2 + side))
+        n = crossed.index(c)
+        if c in direct:
+            return remote(rows_v[c].at[near * 2 + 1 - side], back_n[c], s_near.at[n], r_back_n.at[n], ep_id(near * 2 + 1 - side))
+        return remote(hop_n[c], back_n[c], s_near.at[n], r_back_n.at[n], ep_id(near * 2 + side))
 
     def near_arrival(c):
-        return remote(back_n[c], back_n[c], s_near.at[c], r_back_n.at[c], ep_id(end * 2 + side))
+        n = crossed.index(c)
+        return remote(back_n[c], back_n[c], s_near.at[n], r_back_n.at[n], ep_id(end * 2 + side))
 
     def back_reply():
         return remote(rst_r, rbuf_r, s_rr, r_rr, ep_id(far * 2 + side))
@@ -175,18 +180,33 @@
     def reply(j):
         return remote(rst.at[j], rbuf.at[me], s_rep, r_rep, ep_id(j))
 
-    def st_copy(q, way, dev):
-        return remote(st_z.at[q], st_z.at[q], s_st.at[way], r_st.at[q], ep_id(dev))
-
-    def st_right(q):
-        return st_copy(q, 0, me + 2)
-
-    def st_left(q):
-        return st_copy(q, 1, me - 2)
-
-    def st_mate(at):
-        return remote(st_m.at[at], st_m.at[at], s_st.at[2], r_st.at[line], ep_id(mate))
-
+    def se_copy(s):
+        return remote(st_ep.at[me], st_ep.at[me], s_se, r_se, ep_id(ep_peer(s)))
+
+    def se_all():
+        return remote(st_ep.at[pl.ds(0, ep - 1)], st_ep.at[pl.ds(0, ep - 1)], s_se, r_se, ep_id(mate))
+
+    def say_ready(n):
+        def tell(dev):
+            pl.semaphore_signal(s_ready.at[n], inc=1, device_id=ep_id(dev), device_id_type=MESH)
+
+        @pl.when(pos < last)
+        def _():
+            tell(me + 2)
+
+        @pl.when(pos > 0)
+        def _():
+            tell(me - 2)
+
+        tell(mate)
+
+    def hear_ready(n):
+        pl.semaphore_wait(s_ready.at[n], 1 + (pos < last).astype(jnp.int32) + (pos > 0).astype(jnp.int32))
+        if n + 1 < last:
+            say_ready(n + 1)
+
+    if last > 0:
+        say_ready(0)
     for copy in own:
         copy.wait()
     idx_here.wait()
@@ -321,9 +341,10 @@
         return ((pos - s, left, True), (pos + s, right, False))
 
     def closes(s, c, tail, finish, q):
-        if s == 1 and len(late) and finish is done_block:
+        if s == 1 and len(late):
+            ends = [n for n in late if finish is done_block or n not in crossed]
             if tail:
-                if c == late[-1]:
+                if c == ends[-1]:
                     finish(q)
             elif c == chunks - 1:
                 @pl.when(jnp.logical_not(at_end))
@@ -370,8 +391,13 @@
                         for n in late:
                             step(pos, n).start()
 
-                if not tail:
+                if not (tail and c in crossed):
                     give_leaf(q, c)
+                if s == last - 1 and c == chunks - 1 and len(held):
+                    @pl.when(pos < last if rightward else pos > 0)
+                    def _():
+                        for n in held:
+                            give_leaf(pos, n)
 
     def use(s, c, tail=False):
         for q, ok, rightward in meets(s, c, tail):
@@ -388,21 +414,32 @@
                         if c == swapped[-1]:
                             rst_r[...] = acc_r[...]
                             back_reply().start()
-                            for n in late:
+                            for n in crossed:
                                 near_arrival(n).wait_recv()
                                 acc_n[...] += gathered(back_n[n][...], xb[n][pos], tgt_n[...], tok_dev)
 
-    def take(s, c):
+    def take(s, c, tail=False):
         if s == 0:
-            use_leaf(pos, c)
-            if c == chunks - 1:
-                done_leaf(pos)
+            if len(held) and (c in held or c == chunks - 1):
+                if c not in held:
+                    use_leaf(pos, c)
+
+                @pl.when(near_end if tail else jnp.logical_not(near_end))
+                def _():
+                    if c in held:
+                        use_leaf(pos, c)
+                    if c == (held[-1] if tail else chunks - 1):
+                        done_leaf(pos)
+            else:
+                use_leaf(pos, c)
+                if c == chunks - 1:
+                    done_leaf(pos)
             return
-        for q, ok, _ in meets(s, c, False):
+        for q, ok, _ in meets(s, c, tail):
             @pl.when(ok)
             def _(q=q):
                 use_leaf(q, c)
-                closes(s, c, False, done_leaf, q)
+                closes(s, c, tail, done_leaf, q)
 
     def settle(s, c):
         if c == 0:
@@ -415,19 +452,21 @@
             if c in swapped:
                 hop_rows(c).wait_recv()
                 send_back(1, c).start()
-            if c in late:
+            if c in crossed and c not in direct:
                 hop_near(c).wait_recv()
                 send_near(c).start()
 
     def sort_step(c):
         sort_rows(c)
-        if c in swapped or c in late:
+        if c in swapped or c in crossed:
             @pl.when(at_end)
             def _():
                 if c in swapped:
                     hop_rows(c).start()
                     send_back(0, c).start()
-                if c in late:
+                if c in direct:
+                    send_near(c).start()
+                elif c in crossed:
                     hop_near(c).start()
         use_block(pos, c)
         if c == chunks - 1:
@@ -476,49 +515,37 @@
             tk_copy(s).start()
         tkr[md] = tks[md]
 
-    def pair_stats():
+    def share_stats():
         sd_all().wait_recv()
         total = st_dp[0]
         for d in range(1, dp):
             total = total + st_dp[d]
-        st_m[side] = total
-        st_mate(side).start()
-
-    def share_stats():
-        st_mate(1 - side).wait_recv()
-        st_z[pos] = st_m[0] + st_m[1]
-
-        @pl.when(pos < last)
-        def _():
-            st_right(pos).start()
-
-        @pl.when(pos > 0)
-        def _():
-            st_left(pos).start()
-
-    def pass_stats(s):
-        for q, ok, rightward in ((pos - s, pos - s >= 0, True), (pos + s, pos + s < line, False)):
-            @pl.when(ok)
-            def _(q=q, rightward=rightward):
-                step = st_right if rightward else st_left
-                step(q).wait_recv()
-
-                @pl.when(pos < last if rightward else pos > 0)
-                def _():
-                    step(q).start()
+        st_ep[me] = total
+        loop_ep(lambda s: se_copy(s).start())
 
     plan_block(pos)
     for c in every:
-        give_leaf(pos, c)
+        if c in held:
+            @pl.when(jnp.logical_not(near_end))
+            def _():
+                give_leaf(pos, c)
+        else:
+            give_leaf(pos, c)
     rows_copy.wait()
     for c in every:
         if c == max(chunks - 2, 0):
             learn(1)
             arrive(1, 0)
         sort_step(c)
+        if c < last:
+            hear_ready(c)
+    for n in range(chunks, last):
+        hear_ready(n)
     steps = [(0, c) for c in every] + [(s, c) for s in range(1, line) for c in every]
-    taken = 0
+    taken, tails = 0, []
     for n, (s, c) in enumerate(steps):
+        if s == last and c in swapped:
+            break
         if s > 0:
             if c == 0:
                 if s > 1:
@@ -526,16 +553,14 @@
             if (s, c) != (1, 0):
                 arrive(s, c)
             use(s, c)
-            if s == 2 and (c in swapped or c in late):
-                pass_rows(c)
-            if s == 2 and c == chunks - 1:
-                pass_stats(1)
+            if (s, c) == (2, 0):
+                for n in every:
+                    if n in swapped or n in crossed:
+                        pass_rows(n)
             if (s, c) == (1, 1 if chunks > 1 else 0):
                 route()
                 share_tokens()
-            if (s, c) == (1, max(chunks - 2, 0)):
-                pair_stats()
-            if (s, c) == ((2, 0) if last > 1 else (1, chunks - 1)):
+            if (s, c) == (1, chunks - 1):
                 share_stats()
             while taken <= n - LAG:
                 settle(*steps[taken])
@@ -543,17 +568,23 @@
     for c in late:
         arrive(1, c, True)
         use(1, c, True)
+        for step in steps[taken:taken + 2]:
+            settle(*step)
+        taken = min(taken + 2, len(steps))
+        if c not in crossed:
+            tails.append(c)
     for step in steps[taken:]:
         settle(*step)
-    for s in range(2 if last > 1 else 1, line):
-        pass_stats(s)
-    stats = st_z[0]
-    for q in range(1, line):
-        stats = stats + st_z[q]
+    for c in held:
+        take(0, c, True)
+    for c in tails:
+        take(1, c, True)
+    se_all().wait_recv()
+    stats = lax.fori_loop(1, ep, lambda j, acc: acc + st_ep[j], st_ep[0])
     share = stats[0:1, :] / (token_total * chosen)
     mean = stats[1:2, :] / token_total
     loss_v[...] = experts * jnp.sum(share * mean, axis=1, keepdims=True)
-    loss_copy = pltpu.make_async_copy(loss_v, loss_out, s_out.at[0])
+    loss_copy = pltpu.make_async_copy(loss_v, loss_out, s_out)
     loss_copy.start()
     push_row = scale_v[...] * experts * share
     push = upright(push_row)
@@ -591,11 +622,9 @@
         lg_copy(s).start()
     for c in every:
         at = slice(starts[c], starts[c] + widths[c])
-        tg_v[:, at] = lax.dot_general(
+        tg_out[:, at] = lax.dot_general(
             grad, wt_v[:, at], (((0,), (0,)), ((), ())), preferred_element_type=F32
         ).astype(BF16)
-    tg_store = pltpu.make_async_copy(tg_v, tg_out, s_out.at[1])
-    tg_store.start()
     tk_all().wait_recv()
     lg_all().wait_recv()
     term = dot_nn(lgd[0], tkr[0])
@@ -622,26 +651,26 @@
 
     ups = jnp.where(pos < last, pos + 1, 0)
     downs = jnp.where(pos > 0, line - pos, 0)
-    for buf, sem in ((idx_all, s_idx), (st_z, s_st)):
-        sent(buf, sem.at[0], ups)
-        sent(buf, sem.at[1], downs)
+    sent(idx_all, s_idx.at[0], ups)
+    sent(idx_all, s_idx.at[1], downs)
     sent(idx_all, s_idx.at[2], line)
-    st_mate(side).wait_send()
+    se_all().wait_send()
     for c in every:
         short = 1 if c in swapped else 0
         sent(xb[c], s_right.at[c], ups - jnp.where(pos == last - 1, short, 0))
         sent(xb[c], s_left.at[c], downs - jnp.where(pos == 1, short, 0))
-        skipped = short + (1 if c in late else 0)
+        skipped = short + (1 if c in crossed else 0)
         sent(lsend[c], s_leaf.at[c], line - jnp.where(at_end, skipped, 0))
     if len(swapped):
         @pl.when(at_end)
         def _():
             for c in swapped:
                 piece = rows_v[c].at[pl.ds(0, 3)]
-                remote(piece, piece, s_back.at[c], s_back.at[c], ep_id(mate)).wait_send()
-            for c in late:
-                piece = rows_v[c].at[pl.ds(0, 2)]
-                remote(piece, piece, s_near.at[c], s_near.at[c], ep_id(mate)).wait_send()
+                sem = s_back.at[swapped.index(c)]
+                remote(piece, piece, sem, sem, ep_id(mate)).wait_send()
+            for n, c in enumerate(crossed):
+                piece = rows_v[c].at[pl.ds(0, 1 if c in direct else 2)]
+                remote(piece, piece, s_near.at[n], s_near.at[n], ep_id(mate)).wait_send()
 
         @pl.when(near_end)
         def _():
@@ -651,23 +680,19 @@
     tk_all().wait_send()
     lg_all().wait_send()
     loss_copy.wait()
-    tg_store.wait()
     w_all().wait_recv()
     out = lax.fori_loop(1, ep, lambda j, acc: acc + wr[j], wr[0])
-    wg_v[...] = out / math.sqrt(token_total)
-    wg_copy = pltpu.make_async_copy(wg_v, wg_out, s_out.at[2])
-    wg_copy.start()
+    wg_out[...] = out / math.sqrt(token_total)
     w_all().wait_send()
-    wg_copy.wait()
 
 
 def cut(width):
     if width <= 3 * CHUNK + CHUNK // 2 or width > 4 * CHUNK:
         widths = tuple(min(CHUNK, width - s) for s in range(0, width, CHUNK))
-        return widths, tuple(sum(widths[:c]) for c in range(len(widths))), (), ()
+        return widths, tuple(sum(widths[:c]) for c in range(len(widths))), (), (), (), (), ()
     half = CHUNK // 2
     rest = width - 3 * CHUNK - half
-    return (CHUNK, rest, half, CHUNK, CHUNK), (0, width - rest, CHUNK, CHUNK + half, 2 * CHUNK + half), (2, 3, 4), (2, 1)
+    return (CHUNK, rest, half, CHUNK, CHUNK), (0, width - rest, CHUNK, CHUNK + half, 2 * CHUNK + half), (2, 3, 4), (4, 2, 1), (2, 1), (2,), (3,)
 
 
 def on_device(tokens, out_grad, indices, expert_rows, router_weight, router_bias, balance_scale):
@@ -679,14 +704,15 @@
     dp = lax.axis_size("dp")
     line = ep // 2
     packed = -(-min(tok_dev, (exp_dev - 1) * cap) // 16) * 16
-    widths, starts, swapped, late = cut(width)
+    widths, starts, swapped, late, crossed, direct, held = cut(width)
     chunks = len(widths)
     if line < 4:
-        swapped, late = (), ()
-    cfg = (ep, dp, tok_dev, chosen, experts, exp_dev, cap, packed, widths, starts, swapped, late, tok_dev * ep * dp)
+        swapped, late, crossed, direct, held = (), (), (), (), ()
+    cfg = (ep, dp, tok_dev, chosen, experts, exp_dev, cap, packed, widths, starts, swapped, late, crossed, direct, held, tok_dev * ep * dp)
     part = width // dp
     rows_t = jnp.transpose(expert_rows[0], (0, 2, 1, 3)).reshape(exp_dev, cap * ep, width)
     hbm = pl.BlockSpec(memory_space=pl.ANY)
+    vmem = pl.BlockSpec(memory_space=pltpu.VMEM)
     dma = pltpu.SemaphoreType.DMA
     scratch = [pltpu.VMEM((line, tok_dev, w), BF16) for w in widths]
     scratch += [pltpu.VMEM((line, packed, w), BF16) for w in widths]
@@ -703,18 +729,16 @@
         pltpu.VMEM((1, 1), F32),
         dma((5,)),
         pltpu.VMEM((1, 1), F32),
-        pltpu.VMEM((exp_dev, part), F32),
-        dma((3,)),
+        dma,
         pltpu.VMEM((exp_dev, cap * ep, width), BF16),
         pltpu.VMEM((exp_dev, ep * (-(-cap // 8) * 8), max(widths)), F32),
         pltpu.VMEM((2, 8, tok_dev), F32),
         pltpu.VMEM((2, 8, tok_dev), F32),
         pltpu.VMEM((2, 8, tok_dev), F32),
         pltpu.VMEM((2, 8, tok_dev), F32),
-        dma((chunks,)), dma((chunks,)), dma((chunks,)), dma((chunks,)), dma((chunks,)), dma((chunks,)), dma, dma,
+        *[dma((max(len(swapped), 1),))] * 3, *[dma((max(len(crossed), 1),))] * 3, dma, dma,
         pltpu.VMEM((8, tok_dev), F32),
         pltpu.VMEM((8, tok_dev), F32),
-        pltpu.VMEM((tok_dev, width), BF16),
         pltpu.VMEM((ep, chosen, tok_dev), jnp.int32),
         pltpu.VMEM((line, packed, tok_dev), BF16),
         pltpu.VMEM((line, packed, tok_dev), BF16),
@@ -730,27 +754,26 @@
         pltpu.VMEM((experts, tok_dev), F32),
         pltpu.VMEM((experts, tok_dev), F32),
         pltpu.VMEM((dp, 8, experts), F32),
-        pltpu.VMEM((2, 8, experts), F32),
-        pltpu.VMEM((line, 8, experts), F32),
+        pltpu.VMEM((ep, 8, experts), F32),
         pltpu.VMEM((dp, experts, tok_dev), BF16),
         pltpu.VMEM((ep, exp_dev, part), F32),
         pltpu.VMEM((ep, exp_dev, part), F32),
         dma, dma((chunks,)), dma((3,)), dma((ep,)),
-        dma((chunks,)), dma((chunks,)), dma((line, chunks)),
+        dma((chunks,)), dma((chunks,)), dma((max(line - 1, 1), chunks)),
         dma((chunks,)), dma((line, chunks)), dma, dma,
-        dma, dma, dma, dma, dma((3,)), dma((line + 1,)),
+        dma, dma, dma, dma, dma, dma, pltpu.SemaphoreType.REGULAR((max(line - 1, 1),)),
         dma, dma, dma, dma,
     ]
     token_grad, wg, loss = pl.pallas_call(
         functools.partial(kernel, cfg),
         name="router_backward",
         out_shape=(
-            jax.ShapeDtypeStruct((tok_dev, width), BF16),
-            jax.ShapeDtypeStruct((exp_dev, part), F32),
+            pltpu.VMEM((tok_dev, width), BF16),
+            pltpu.VMEM((exp_dev, part), F32),
             jax.ShapeDtypeStruct((1, 1), F32),
         ),
         in_specs=[hbm] * 7,
-        out_specs=(hbm,) * 3,
+        out_specs=(vmem, vmem, hbm),
         scratch_shapes=scratch,
         compiler_params=pltpu.CompilerParams(
             collective_id=0, has_side_effects=True, vmem_limit_bytes=56 * 1024 * 1024

time: 87.2 us -> 82.9 us (0.951)
  Pallas kernels: 81 us -> 78.1 us
  local copies, waits for them, and re-layouts: 2.94 us -> 1.6 us
    pallas_call x1, Pallas kernels: 81 us -> 78.1 us  [on_device(): pl.pallas_call(functools.partial(kernel, cfg), name='router_backward', ou...]
    unnamed x4 -> x2, local copies, waits for them, and re-layouts: 2.94 us -> 1.6 us
where the time goes in v2:
time: 82.9 us; the launch traced here: 82.7 us
  Pallas kernels  78.1 us (94%)
  between operations  2.98 us (4%)
  local copies, waits for them, and re-layouts  1.6 us (2%)
    pallas_call x1, Pallas kernels, on_device(): pl.pallas_call(functools.partial(kernel, cfg), name='router_backward', ou...  78.1 us

profile of v2, /device:TPU:0, one launch (start us, length us, event | category | flops | bytes accessed | tf_op | source)
XLA Modules:
  0.0 82.7 jit_solution(13734336744763712162)
XLA Ops:
  1.3 78.1 %router_backward.1 = (bf16[192,2880]{1,0:T(8,128)(2,1)S(1)}, f32[4,720]{1,0:T(4,128)S(1)}, f32[1,1]{1,0:T(1,128)}) custom-call(s32[4,192]{1,0:T(4,128)} %bitcast.15, bf16[192,2880]{1,0:T(8,128)(2,1)} %refs_1_.1, bf16[4,288,2880]{2,1,0:T(8,128)(2,1)} %bitcast.13, bf16[192,2880]{1,0:T(8,128)(2,1)} %refs_3_.1, bf16[32,2880]{1,0:T(8,128)(2,1)} %bitcast.14, ...), custom_call_target="tpu_custom_call" | custom-call | tf_op jit(solution)/shard_map/router_backward/pallas_call | solution.py:767
  79.4 1.0 %copy.13 = bf16[192,2880]{1,0:T(8,128)(2,1)} copy(bf16[192,2880]{1,0:T(8,128)(2,1)S(1)} %get-tuple-element.9) | data formatting | bytes 2211840
  80.4 0.6 copy.14

commit v3 on v2

--- a/solution.py
+++ b/solution.py
@@ -27,8 +27,22 @@
     )
 
 
+def fold(left, right):
+    half = right.shape[0] // 2
+    pieces = [left, jnp.concatenate([right[0:half], right[half:]], axis=1)]
+    short = -3 * half % 16
+    if short:
+        pieces.append(jnp.zeros((short, 128), F32))
+    return jnp.concatenate(pieces, axis=0)
+
+
+def unfold(x, rows):
+    low = x[rows:, :].astype(F32)[0:rows // 2]
+    return x[0:rows], jnp.concatenate([low[:, 0:64], low[:, 64:128]], axis=0).astype(BF16)
+
+
 def kernel(cfg, *refs):
-    (ep, dp, tok_dev, chosen, experts, exp_dev, cap, packed, widths, starts, swapped, late, crossed, direct, held, token_total) = cfg
+    (ep, dp, tok_dev, chosen, experts, exp_dev, cap, packed, widths, starts, swapped, late, crossed, direct, held, folded, token_total) = cfg
     line = ep // 2
     last = line - 1
     chunks = len(widths)
@@ -44,7 +58,7 @@
     lrecv = refs[2 * chunks:3 * chunks]
     rows_v = refs[3 * chunks:4 * chunks]
     back = refs[4 * chunks:5 * chunks]
-    (tok_v, wt_v, bias_v, scale_v, s_in, loss_v, s_out,
+    (tok_v, wt_v, bias_v, scale_v, s_in, loss_v, s_out, stage,
      rows_raw, piled, tgt_r, acc_r, rst_r, rbuf_r, s_back, r_back, r_hop, s_near, r_hop_n, r_back_n, s_rr, r_rr, tgt_n, acc_n,
      idx_all, pin, pout, tgt_x, tgt_p, acc_x, acc_p, rst, rbuf, tks, tkr, logit_v, prob_v,
      named_v, st_dp, st_ep, lgd, ws, wr,
@@ -94,7 +108,9 @@
 
     idx_here = pltpu.make_async_copy(idx_in, idx_all.at[me], s_in.at[0])
     own = [
-        pltpu.make_async_copy(grad_in.at[:, pl.ds(starts[c], widths[c])], xb[c].at[pos], s_own.at[c])
+        pltpu.make_async_copy(
+            grad_in.at[:, pl.ds(starts[c], widths[c])], stage if c in folded else xb[c].at[pos], s_own.at[c]
+        )
         for c in every
     ]
     rows_copy = pltpu.make_async_copy(rows_in, rows_raw, s_rows)
@@ -221,6 +237,9 @@
 
     idx_mate(pos).start()
     for c in every:
+        if c in folded:
+            xb[c][pos] = fold(stage[:, 0:128].astype(F32), stage[:, 128:192].astype(F32)).astype(BF16)
+
         @pl.when(pos < last - (c in late))
         def _():
             to_right(pos, c).start()
@@ -278,7 +297,7 @@
     deep = piled.shape[1] // ep
     slot_r = lax.broadcasted_iota(jnp.int32, (deep, cap * ep), 0)
     lies = lax.broadcasted_iota(jnp.int32, (deep, cap * ep), 1)
-    spare = rows_v[0].shape[1] - exp_dev * cap
+    spare = -exp_dev * cap % 16
 
     def sort_rows(c):
         w = widths[c]
@@ -293,16 +312,25 @@
             pieces = [piled[e, at, 0:w][0:cap, :] for e in range(exp_dev)]
             if spare:
                 pieces.append(jnp.zeros((spare, w), F32))
-            rows_v[c][j] = jnp.concatenate(pieces, axis=0).astype(BF16)
+            block = jnp.concatenate(pieces, axis=0)
+            if c in folded:
+                block = fold(block[:, 0:128], block[:, 128:192])
+            rows_v[c][j] = block.astype(BF16)
             return carry
 
         lax.fori_loop(0, ep, put, 0)
 
-    def gathered(table, block, target, count):
-        height = table.shape[0]
+    def all_dots(c, table, block, count):
+        if c not in folded:
+            return dot_nt(table, block)
+        (table_l, table_r), (block_l, block_r) = unfold(table, exp_dev * cap + spare), unfold(block, count)
+        return dot_nt(table_l, block_l) + dot_nt(table_r, block_r)
+
+    def gathered(c, table, block, target, count):
+        dots = all_dots(c, table, block, count)
+        height = dots.shape[0]
         slot = lax.broadcasted_iota(jnp.int32, (height, count), 0).astype(F32)
         row = lax.broadcasted_iota(jnp.int32, (8, count), 0)
-        dots = dot_nt(table, block)
         out = jnp.zeros((8, count), F32)
         for e in range(exp_dev):
             want = jnp.where(target[e:e + 1, :] >= 0.0, target[e:e + 1, :] + e * cap, -1.0)
@@ -311,15 +339,19 @@
         return out
 
     def give_leaf(q, c):
-        lsend[c][q] = dot_nn(pout[q], xb[c][q]).astype(BF16)
+        if c in folded:
+            left, right = unfold(xb[c][q], tok_dev)
+            lsend[c][q] = fold(dot_nn(pout[q], left), dot_nn(pout[q], right)).astype(BF16)
+        else:
+            lsend[c][q] = dot_nn(pout[q], xb[c][q]).astype(BF16)
         leaf(q, c).start()
 
     def use_block(q, c):
-        acc_x[q] += gathered(rows_v[c][q * 2 + side], xb[c][q], tgt_x[q], tok_dev)
+        acc_x[q] += gathered(c, rows_v[c][q * 2 + side], xb[c][q], tgt_x[q], tok_dev)
 
     def use_leaf(q, c):
         leaf(q, c).wait_recv()
-        acc_p[q] += gathered(rows_v[c][q * 2 + 1 - side], lrecv[c][q], tgt_p[q], packed)
+        acc_p[q] += gathered(c, rows_v[c][q * 2 + 1 - side], lrecv[c][q], tgt_p[q], packed)
 
     def answer(j, value):
         rst[j] = value
@@ -410,13 +442,13 @@
                     def _():
                         back_arrival(c).wait_recv()
                         for b in range(2):
-                            acc_r[b] += gathered(back[c][b], xb[c][q], tgt_r[b], tok_dev)
+                            acc_r[b] += gathered(c, back[c][b], xb[c][q], tgt_r[b], tok_dev)
                         if c == swapped[-1]:
                             rst_r[...] = acc_r[...]
                             back_reply().start()
                             for n in crossed:
                                 near_arrival(n).wait_recv()
-                                acc_n[...] += gathered(back_n[n][...], xb[n][pos], tgt_n[...], tok_dev)
+                                acc_n[...] += gathered(n, back_n[n][...], xb[n][pos], tgt_n[...], tok_dev)
 
     def take(s, c, tail=False):
         if s == 0:
@@ -565,12 +597,16 @@
             while taken <= n - LAG:
                 settle(*steps[taken])
                 taken += 1
-    for c in late:
+    for m, c in enumerate(late):
+        if m == 0 and taken < len(steps):
+            settle(*steps[taken])
+            taken += 1
         arrive(1, c, True)
         use(1, c, True)
-        for step in steps[taken:taken + 2]:
-            settle(*step)
-        taken = min(taken + 2, len(steps))
+        if m == 0:
+            while taken < len(steps) and not (steps[taken][0] == last and steps[taken][1] in swapped):
+                settle(*steps[taken])
+                taken += 1
         if c not in crossed:
             tails.append(c)
     for step in steps[taken:]:
@@ -686,6 +722,14 @@
     w_all().wait_send()
 
 
+def finish(tg_in, wg_in, tg_out, wg_out, sems):
+    copies = [pltpu.make_async_copy(tg_in, tg_out, sems.at[0]), pltpu.make_async_copy(wg_in, wg_out, sems.at[1])]
+    for copy in copies:
+        copy.start()
+    for copy in copies:
+        copy.wait()
+
+
 def cut(width):
     if width <= 3 * CHUNK + CHUNK // 2 or width > 4 * CHUNK:
         widths = tuple(min(CHUNK, width - s) for s in range(0, width, CHUNK))
@@ -708,20 +752,24 @@
     chunks = len(widths)
     if line < 4:
         swapped, late, crossed, direct, held = (), (), (), (), ()
-    cfg = (ep, dp, tok_dev, chosen, experts, exp_dev, cap, packed, widths, starts, swapped, late, crossed, direct, held, tok_dev * ep * dp)
     part = width // dp
     rows_t = jnp.transpose(expert_rows[0], (0, 2, 1, 3)).reshape(exp_dev, cap * ep, width)
     hbm = pl.BlockSpec(memory_space=pl.ANY)
     vmem = pl.BlockSpec(memory_space=pltpu.VMEM)
     dma = pltpu.SemaphoreType.DMA
-    scratch = [pltpu.VMEM((line, tok_dev, w), BF16) for w in widths]
-    scratch += [pltpu.VMEM((line, packed, w), BF16) for w in widths]
-    scratch += [pltpu.VMEM((line, packed, w), BF16) for w in widths]
-    scratch += [pltpu.VMEM((ep, -(-exp_dev * cap // 16) * 16, w), BF16) for w in widths]
-    scratch += [pltpu.VMEM((2, -(-exp_dev * cap // 16) * 16, w), BF16) for w in widths]
-    scratch += [pltpu.VMEM((-(-exp_dev * cap // 16) * 16, w), BF16) for w in widths]
-    scratch += [pltpu.VMEM((-(-exp_dev * cap // 16) * 16, w), BF16) for w in widths]
-    scratch += [pltpu.VMEM((-(-exp_dev * cap // 16) * 16, w), BF16) for w in widths]
+    height = -(-exp_dev * cap // 16) * 16
+    folded = tuple(c for c in late if widths[c] == 192 and tok_dev % 16 == 0)
+
+    def room(*shape):
+        rows = shape[-1]
+        return [
+            pltpu.VMEM(shape[:-1] + ((-(-rows * 3 // 32) * 16, 128) if c in folded else (rows, w)), BF16)
+            for c, w in enumerate(widths)
+        ]
+
+    cfg = (ep, dp, tok_dev, chosen, experts, exp_dev, cap, packed, widths, starts, swapped, late, crossed, direct, held, folded, tok_dev * ep * dp)
+    scratch = room(line, tok_dev) + room(line, packed) + room(line, packed) + room(ep, height)
+    scratch += room(2, height) + room(height) + room(height) + room(height)
     scratch += [
         pltpu.VMEM((tok_dev, width), BF16),
         pltpu.VMEM((experts, width), BF16),
@@ -730,6 +778,7 @@
         dma((5,)),
         pltpu.VMEM((1, 1), F32),
         dma,
+        pltpu.VMEM((tok_dev, 192), BF16),
         pltpu.VMEM((exp_dev, cap * ep, width), BF16),
         pltpu.VMEM((exp_dev, ep * (-(-cap // 8) * 8), max(widths)), F32),
         pltpu.VMEM((2, 8, tok_dev), F32),
@@ -779,6 +828,17 @@
             collective_id=0, has_side_effects=True, vmem_limit_bytes=56 * 1024 * 1024
         ),
     )(indices.T, out_grad, rows_t, tokens, router_weight.T, router_bias.reshape(1, experts), balance_scale.reshape(1, 1))
+    token_grad, wg = pl.pallas_call(
+        finish,
+        name="write_out",
+        out_shape=(
+            jax.ShapeDtypeStruct(token_grad.shape, token_grad.dtype),
+            jax.ShapeDtypeStruct(wg.shape, wg.dtype),
+        ),
+        in_specs=[vmem, vmem],
+        out_specs=(hbm, hbm),
+        scratch_shapes=[dma((2,))],
+    )(*(pltpu.with_memory_space_constraint(x, pltpu.VMEM) for x in (token_grad, wg)))
     return (token_grad, wg.T, loss.reshape(1))
 
 

time: 82.9 us -> 81.4 us (0.982)
  local copies, waits for them, and re-layouts: 1.6 us -> 0 us
    unnamed x2 -> x0, local copies, waits for them, and re-layouts: 1.6 us -> none
    pallas_call x0 -> x1, Pallas kernels: none -> 1.02 us  [on_device(): pl.pallas_call(finish, name='write_out', out_shape=(jax.ShapeDtypeStruct(...]
    pallas_call x1, Pallas kernels: 78.1 us -> 77.1 us  [on_device(): pl.pallas_call(functools.partial(kernel, cfg), name='router_backward', ou...]
where the time goes in v3:
time: 81.4 us; the launch traced here: 81.2 us
  Pallas kernels  78.2 us (96%)
  between operations  3.05 us (4%)
    pallas_call x1, Pallas kernels, on_device(): pl.pallas_call(functools.partial(kernel, cfg), name='router_backward', ou...  77.1 us

profile of v3, /device:TPU:0, one launch (start us, length us, event | category | flops | bytes accessed | tf_op | source)
XLA Modules:
  0.0 81.2 jit_solution(8045207620682989642)
XLA Ops:
  1.3 77.1 %router_backward.1 = (bf16[192,2880]{1,0:T(8,128)(2,1)S(1)}, f32[4,720]{1,0:T(4,128)S(1)}, f32[1,1]{1,0:T(1,128)}) custom-call(s32[4,192]{1,0:T(4,128)} %bitcast.14, bf16[192,2880]{1,0:T(8,128)(2,1)} %refs_1_.1, bf16[4,288,2880]{2,1,0:T(8,128)(2,1)} %bitcast.12, bf16[192,2880]{1,0:T(8,128)(2,1)} %refs_3_.1, bf16[32,2880]{1,0:T(8,128)(2,1)} %bitcast.13, ...), custom_call_target="tpu_custom_call" | custom-call | tf_op jit(solution)/shard_map/router_backward/pallas_call | solution.py:816
  78.4 1.0 %write_out.1 = (bf16[192,2880]{1,0:T(8,128)(2,1)}, f32[4,720]{1,0:T(4,128)}) custom-call(bf16[192,2880]{1,0:T(8,128)(2,1)S(1)} %get-tuple-element.8.tg_in, f32[4,720]{1,0:T(4,128)S(1)} %get-tuple-element.9.wg_in), custom_call_target="tpu_custom_call" | custom-call | tf_op jit(solution)/shard_map/write_out/pallas_call | solution.py:831

commit v4 on v3

--- a/solution.py
+++ b/solution.py
@@ -60,10 +60,9 @@
     back = refs[4 * chunks:5 * chunks]
     (tok_v, wt_v, bias_v, scale_v, s_in, loss_v, s_out, stage,
      rows_raw, piled, tgt_r, acc_r, rst_r, rbuf_r, s_back, r_back, r_hop, s_near, r_hop_n, r_back_n, s_rr, r_rr, tgt_n, acc_n,
-     idx_all, pin, pout, tgt_x, tgt_p, acc_x, acc_p, rst, rbuf, tks, tkr, logit_v, prob_v,
-     named_v, st_dp, st_ep, lgd, ws, wr,
+     idx_all, pin, pout, tgt_x, tgt_p, acc_x, acc_p, rst, rbuf, tks, tkr, mp, nbuf, st_dp, st_ep, lgd, ws, wr,
      s_rows, s_own, s_idx, r_idx, s_right, s_left, r_x, s_leaf, r_leaf, s_rep, r_rep,
-     s_tk, r_tk, s_sd, r_sd, s_se, r_se, s_ready, s_lg, r_lg, s_w, r_w) = refs[8 * chunks:]
+     s_tk, r_tk, s_sd, r_sd, s_se, r_se, s_ready, s_mp, r_mp, s_nb, r_nb, s_w, r_w) = refs[8 * chunks:]
     me = lax.axis_index("ep")
     md = lax.axis_index("dp")
     pos = me // 2
@@ -187,14 +186,32 @@
         n = crossed.index(c)
         return remote(back_n[c], back_n[c], s_near.at[n], r_back_n.at[n], ep_id(end * 2 + side))
 
-    def back_reply():
-        return remote(rst_r, rbuf_r, s_rr, r_rr, ep_id(far * 2 + side))
-
-    def back_reply_arrival():
-        return remote(rst_r, rbuf_r, s_rr, r_rr, ep_id((last - near) * 2 + side))
-
-    def reply(j):
-        return remote(rst.at[j], rbuf.at[me], s_rep, r_rep, ep_id(j))
+    def back_reply(d):
+        return remote(rst_r, rbuf_r.at[md], s_rr, r_rr, (far * 2 + side, d))
+
+    def back_replies():
+        return remote(rbuf_r, rbuf_r, s_rr, r_rr, ep_id((last - near) * 2 + side))
+
+    def reply(j, d):
+        return remote(rst.at[j], rbuf.at[md * ep + me], s_rep, r_rep, (j, d))
+
+    def replies():
+        piece = rbuf.at[pl.ds(0, ep * dp - 1)]
+        return remote(piece, piece, s_rep, r_rep, ep_id(mate))
+
+    def near_share(s):
+        return remote(nbuf.at[md], nbuf.at[md], s_nb, r_nb, (me, dp_peer(s)))
+
+    def near_shares():
+        piece = nbuf.at[pl.ds(0, dp - 1)]
+        return remote(piece, piece, s_nb, r_nb, (me, dp_peer(1)))
+
+    def mp_copy(s):
+        return remote(mp.at[md], mp.at[md], s_mp, r_mp, (me, dp_peer(s)))
+
+    def mp_all():
+        piece = mp.at[pl.ds(0, dp - 1)]
+        return remote(piece, piece, s_mp, r_mp, (me, dp_peer(1)))
 
     def se_copy(s):
         return remote(st_ep.at[me], st_ep.at[me], s_se, r_se, ep_id(ep_peer(s)))
@@ -354,8 +371,9 @@
         acc_p[q] += gathered(c, rows_v[c][q * 2 + 1 - side], lrecv[c][q], tgt_p[q], packed)
 
     def answer(j, value):
-        rst[j] = value
-        reply(j).start()
+        rst[j] = value[0:exp_dev]
+        for d in range(dp):
+            reply(j, d).start()
 
     def done_block(q):
         answer(q * 2 + side, acc_x[q])
@@ -444,11 +462,15 @@
                         for b in range(2):
                             acc_r[b] += gathered(c, back[c][b], xb[c][q], tgt_r[b], tok_dev)
                         if c == swapped[-1]:
-                            rst_r[...] = acc_r[...]
-                            back_reply().start()
+                            rst_r[...] = acc_r[:, 0:exp_dev, :]
+                            for d in range(dp):
+                                back_reply(d).start()
                             for n in crossed:
                                 near_arrival(n).wait_recv()
                                 acc_n[...] += gathered(n, back_n[n][...], xb[n][pos], tgt_n[...], tok_dev)
+                            nbuf[md] = acc_n[0:exp_dev]
+                            for n in range(1, dp):
+                                near_share(n).start()
 
     def take(s, c, tail=False):
         if s == 0:
@@ -502,7 +524,10 @@
                     hop_near(c).start()
         use_block(pos, c)
         if c == chunks - 1:
-            rbuf[me] = acc_x[pos]
+            rst[me] = acc_x[pos][0:exp_dev]
+            rbuf[md * ep + me] = acc_x[pos][0:exp_dev]
+            for n in range(1, dp):
+                reply(me, dp_peer(n)).start()
 
     part = tok_in.shape[1] // dp
 
@@ -529,9 +554,10 @@
         top = jnp.max(logits, axis=0, keepdims=True)
         power = jnp.exp(logits - top)
         prob = power / jnp.sum(power, axis=0, keepdims=True)
-        logit_v[...] = logits
-        prob_v[...] = prob
-        named_v[...] = named
+        high = jnp.max(jnp.where(named > 0.5, logits, -jnp.inf), axis=0, keepdims=True)
+        mix = jnp.where(named > 0.5, jnp.exp(jnp.minimum(logits - high, 0.0)), 0.0)
+        mp[md, 0] = mix / jnp.sum(mix, axis=0, keepdims=True)
+        mp[md, 1] = prob
         ones = jnp.ones((8, tok_dev), F32)
         count_row = dot_nt(ones, named, lax.Precision.HIGHEST)
         prob_row = dot_nt(ones, prob, lax.Precision.HIGHEST)
@@ -539,6 +565,8 @@
         st_dp[md] = jnp.where(stat_row == 0, count_row, prob_row)
         for s in range(1, dp):
             sd_copy(s).start()
+        for s in range(1, dp):
+            mp_copy(s).start()
 
     def share_tokens():
         for d in range(dp):
@@ -624,45 +652,31 @@
     loss_copy.start()
     push_row = scale_v[...] * experts * share
     push = upright(push_row)
-    prob = prob_v[...]
-    spread = prob * (push - jnp.sum(prob * push, axis=0, keepdims=True))
-    named = named_v[...]
-    logits = logit_v[...]
-    high = jnp.max(jnp.where(named > 0.5, logits, -jnp.inf), axis=0, keepdims=True)
-    mix = jnp.where(named > 0.5, jnp.exp(jnp.minimum(logits - high, 0.0)), 0.0)
-    mix = mix / jnp.sum(mix, axis=0, keepdims=True)
-
-    remote(rst.at[pl.ds(0, ep - 1)], rbuf.at[pl.ds(0, ep - 1)], s_rep, r_rep, ep_id(mate)).wait_recv()
+    mp_all().wait_recv()
+    tk_all().wait_recv()
+    spreads = []
+    for d in range(dp):
+        prob = mp[d, 1]
+        spreads.append(prob * (push - jnp.sum(prob * push, axis=0, keepdims=True)))
+    replies().wait_recv()
     if len(swapped):
         @pl.when(at_end)
         def _():
-            back_reply_arrival().wait_recv()
-            for b in range(2):
-                rbuf[far * 2 + b] += rbuf_r[b]
+            back_replies().wait_recv()
+            for d in range(dp):
+                for b in range(2):
+                    rbuf[d * ep + far * 2 + b] += rbuf_r[d, b]
 
         @pl.when(near_end)
         def _():
-            rbuf[end * 2 + 1 - side] += acc_n[...]
-    dots = jnp.concatenate([rbuf[j, 0:exp_dev, :] for j in range(ep)], axis=0)
-    sel = mix * (dots - jnp.sum(mix * dots, axis=0, keepdims=True))
-    grad = (spread + sel).astype(BF16)
-    lgd[md] = grad
-
-    def lg_copy(s):
-        return remote(lgd.at[md], lgd.at[md], s_lg, r_lg, (me, dp_peer(s)))
-
-    def lg_all():
-        return remote(lgd.at[pl.ds(0, dp - 1)], lgd.at[pl.ds(0, dp - 1)], s_lg, r_lg, (me, dp_peer(1)))
-
-    for s in range(1, dp):
-        lg_copy(s).start()
-    for c in every:
-        at = slice(starts[c], starts[c] + widths[c])
-        tg_out[:, at] = lax.dot_general(
-            grad, wt_v[:, at], (((0,), (0,)), ((), ())), preferred_element_type=F32
-        ).astype(BF16)
-    tk_all().wait_recv()
-    lg_all().wait_recv()
+            near_shares().wait_recv()
+            for d in range(dp):
+                rbuf[d * ep + end * 2 + 1 - side] += nbuf[d]
+    for d in range(dp):
+        mix = mp[d, 0]
+        dots = jnp.concatenate([rbuf[d * ep + j] for j in range(ep)], axis=0)
+        sel = mix * (dots - jnp.sum(mix * dots, axis=0, keepdims=True))
+        lgd[d] = (spreads[d] + sel).astype(BF16)
     term = dot_nn(lgd[0], tkr[0])
     for d in range(1, dp):
         term = term + dot_nn(lgd[d], tkr[d])
@@ -677,6 +691,12 @@
         return remote(ws.at[pl.ds(0, ep - 1)], wr.at[pl.ds(0, ep - 1)], s_w, r_w, ep_id(mate))
 
     loop_ep(lambda s_: w_copy(s_).start())
+    grad = lgd[md]
+    for c in every:
+        at = slice(starts[c], starts[c] + widths[c])
+        tg_out[:, at] = lax.dot_general(
+            grad, wt_v[:, at], (((0,), (0,)), ((), ())), preferred_element_type=F32
+        ).astype(BF16)
 
     def sent(ref, sem, count):
         for n in range(1, line + 1):
@@ -710,11 +730,12 @@
 
         @pl.when(near_end)
         def _():
-            back_reply().wait_send()
-    remote(rst.at[pl.ds(0, ep - 1)], rbuf.at[pl.ds(0, ep - 1)], s_rep, r_rep, ep_id(mate)).wait_send()
+            back_replies().wait_send()
+            near_shares().wait_send()
+    replies().wait_send()
+    mp_all().wait_send()
     sd_all().wait_send()
     tk_all().wait_send()
-    lg_all().wait_send()
     loss_copy.wait()
     w_all().wait_recv()
     out = lax.fori_loop(1, ep, lambda j, acc: acc + wr[j], wr[0])
@@ -783,8 +804,8 @@
         pltpu.VMEM((exp_dev, ep * (-(-cap // 8) * 8), max(widths)), F32),
         pltpu.VMEM((2, 8, tok_dev), F32),
         pltpu.VMEM((2, 8, tok_dev), F32),
-        pltpu.VMEM((2, 8, tok_dev), F32),
-        pltpu.VMEM((2, 8, tok_dev), F32),
+        pltpu.VMEM((2, exp_dev, tok_dev), F32),
+        pltpu.VMEM((dp, 2, exp_dev, tok_dev), F32),
         *[dma((max(len(swapped), 1),))] * 3, *[dma((max(len(crossed), 1),))] * 3, dma, dma,
         pltpu.VMEM((8, tok_dev), F32),
         pltpu.VMEM((8, tok_dev), F32),
@@ -795,13 +816,12 @@
         pltpu.VMEM((line, 8, packed), F32),
         pltpu.VMEM((line, 8, tok_dev), F32),
         pltpu.VMEM((line, 8, packed), F32),
-        pltpu.VMEM((ep, 8, tok_dev), F32),
-        pltpu.VMEM((ep, 8, tok_dev), F32),
+        pltpu.VMEM((ep, exp_dev, tok_dev), F32),
+        pltpu.VMEM((dp * ep, exp_dev, tok_dev), F32),
         pltpu.VMEM((dp, tok_dev, part), BF16),
         pltpu.VMEM((dp, tok_dev, part), BF16),
-        pltpu.VMEM((experts, tok_dev), F32),
-        pltpu.VMEM((experts, tok_dev), F32),
-        pltpu.VMEM((experts, tok_dev), F32),
+        pltpu.VMEM((dp, 2, experts, tok_dev), F32),
+        pltpu.VMEM((dp, exp_dev, tok_dev), F32),
         pltpu.VMEM((dp, 8, experts), F32),
         pltpu.VMEM((ep, 8, experts), F32),
         pltpu.VMEM((dp, experts, tok_dev), BF16),
@@ -811,7 +831,7 @@
         dma((chunks,)), dma((chunks,)), dma((max(line - 1, 1), chunks)),
         dma((chunks,)), dma((line, chunks)), dma, dma,
         dma, dma, dma, dma, dma, dma, pltpu.SemaphoreType.REGULAR((max(line - 1, 1),)),
-        dma, dma, dma, dma,
+        dma, dma, dma, dma, dma, dma,
     ]
     token_grad, wg, loss = pl.pallas_call(
         functools.partial(kernel, cfg),

time: 81.4 us -> 79.6 us (0.978)
  Pallas kernels: 78.2 us -> 76.4 us
    pallas_call x1, Pallas kernels: 77.1 us -> 75.4 us  [on_device(): pl.pallas_call(functools.partial(kernel, cfg), name='router_backward', ou...]
where the time goes in v4:
time: 79.6 us; the launch traced here: 79.4 us
  Pallas kernels  76.4 us (96%)
  between operations  3.05 us (4%)
    pallas_call x1, Pallas kernels, on_device(): pl.pallas_call(functools.partial(kernel, cfg), name='router_backward', ou...  75.4 us

profile of v4, /device:TPU:0, one launch (start us, length us, event | category | flops | bytes accessed | tf_op | source)
XLA Modules:
  0.0 79.4 jit_solution(16373645607536227342)
XLA Ops:
  1.3 75.4 %router_backward.1 = (bf16[192,2880]{1,0:T(8,128)(2,1)S(1)}, f32[4,720]{1,0:T(4,128)S(1)}, f32[1,1]{1,0:T(1,128)}) custom-call(s32[4,192]{1,0:T(4,128)} %bitcast.14, bf16[192,2880]{1,0:T(8,128)(2,1)} %refs_1_.1, bf16[4,288,2880]{2,1,0:T(8,128)(2,1)} %bitcast.12, bf16[192,2880]{1,0:T(8,128)(2,1)} %refs_3_.1, bf16[32,2880]{1,0:T(8,128)(2,1)} %bitcast.13, ...), custom_call_target="tpu_custom_call" | custom-call | tf_op jit(solution)/shard_map/router_backward/pallas_call | solution.py:836
  76.7 1.0 %write_out.1 = (bf16[192,2880]{1,0:T(8,128)(2,1)}, f32[4,720]{1,0:T(4,128)}) custom-call(bf16[192,2880]{1,0:T(8,128)(2,1)S(1)} %get-tuple-element.8.tg_in, f32[4,720]{1,0:T(4,128)S(1)} %get-tuple-element.9.wg_in), custom_call_target="tpu_custom_call" | custom-call | tf_op jit(solution)/shard_map/write_out/pallas_call | solution.py:851

commit v5 on v4

--- a/solution.py
+++ b/solution.py
@@ -455,22 +455,22 @@
             def _(q=q, rightward=rightward):
                 use_block(q, c)
                 closes(s, c, tail, done_block, q)
-                if s == last - 1 and c in swapped:
+                if s == last - 1 and len(swapped) and c == chunks - 1:
                     @pl.when(pos < last if rightward else pos > 0)
                     def _():
-                        back_arrival(c).wait_recv()
-                        for b in range(2):
-                            acc_r[b] += gathered(c, back[c][b], xb[c][q], tgt_r[b], tok_dev)
-                        if c == swapped[-1]:
-                            rst_r[...] = acc_r[:, 0:exp_dev, :]
-                            for d in range(dp):
-                                back_reply(d).start()
-                            for n in crossed:
-                                near_arrival(n).wait_recv()
-                                acc_n[...] += gathered(n, back_n[n][...], xb[n][pos], tgt_n[...], tok_dev)
-                            nbuf[md] = acc_n[0:exp_dev]
-                            for n in range(1, dp):
-                                near_share(n).start()
+                        for m in swapped:
+                            back_arrival(m).wait_recv()
+                            for b in range(2):
+                                acc_r[b] += gathered(m, back[m][b], xb[m][q], tgt_r[b], tok_dev)
+                        rst_r[...] = acc_r[:, 0:exp_dev, :]
+                        for d in range(dp):
+                            back_reply(d).start()
+                        for n in crossed:
+                            near_arrival(n).wait_recv()
+                            acc_n[...] += gathered(n, back_n[n][...], xb[n][pos], tgt_n[...], tok_dev)
+                        nbuf[md] = acc_n[0:exp_dev]
+                        for n in range(1, dp):
+                            near_share(n).start()
 
     def take(s, c, tail=False):
         if s == 0:
@@ -613,9 +613,9 @@
             if (s, c) != (1, 0):
                 arrive(s, c)
             use(s, c)
-            if (s, c) == (2, 0):
+            if s == 2:
                 for n in every:
-                    if n in swapped or n in crossed:
+                    if (n in swapped or n in crossed) and c == (0 if n < 3 else n - 1):
                         pass_rows(n)
             if (s, c) == (1, 1 if chunks > 1 else 0):
                 route()
@@ -757,7 +757,7 @@
         return widths, tuple(sum(widths[:c]) for c in range(len(widths))), (), (), (), (), ()
     half = CHUNK // 2
     rest = width - 3 * CHUNK - half
-    return (CHUNK, rest, half, CHUNK, CHUNK), (0, width - rest, CHUNK, CHUNK + half, 2 * CHUNK + half), (2, 3, 4), (4, 2, 1), (2, 1), (2,), (3,)
+    return (CHUNK, rest, half, CHUNK, CHUNK), (0, width - rest, CHUNK, CHUNK + half, 2 * CHUNK + half), (2, 3, 4), (4, 2, 1), (2, 1), (2,), (4,)
 
 
 def on_device(tokens, out_grad, indices, expert_rows, router_weight, router_bias, balance_scale):

time: 79.6 us -> 79.6 us (level)
  no operation moved by 1% of the time
where the time goes in v5:
time: 79.6 us; the launch traced here: 79.4 us
  Pallas kernels  76.4 us (96%)
  between operations  3.05 us (4%)
    pallas_call x1, Pallas kernels, on_device(): pl.pallas_call(functools.partial(kernel, cfg), name='router_backward', ou...  75.4 us

profile of v5, /device:TPU:0, one launch (start us, length us, event | category | flops | bytes accessed | tf_op | source)
XLA Modules:
  0.0 79.4 jit_solution(2526009641688124585)
XLA Ops:
  1.3 75.4 %router_backward.1 = (bf16[192,2880]{1,0:T(8,128)(2,1)S(1)}, f32[4,720]{1,0:T(4,128)S(1)}, f32[1,1]{1,0:T(1,128)}) custom-call(s32[4,192]{1,0:T(4,128)} %bitcast.14, bf16[192,2880]{1,0:T(8,128)(2,1)} %refs_1_.1, bf16[4,288,2880]{2,1,0:T(8,128)(2,1)} %bitcast.12, bf16[192,2880]{1,0:T(8,128)(2,1)} %refs_3_.1, bf16[32,2880]{1,0:T(8,128)(2,1)} %bitcast.13, ...), custom_call_target="tpu_custom_call" | custom-call | tf_op jit(solution)/shard_map/router_backward/pallas_call | solution.py:836
  76.7 1.0 %write_out.1 = (bf16[192,2880]{1,0:T(8,128)(2,1)}, f32[4,720]{1,0:T(4,128)}) custom-call(bf16[192,2880]{1,0:T(8,128)(2,1)S(1)} %get-tuple-element.8.tg_in, f32[4,720]{1,0:T(4,128)S(1)} %get-tuple-element.9.wg_in), custom_call_target="tpu_custom_call" | custom-call | tf_op jit(solution)/shard_map/write_out/pallas_call | solution.py:851
